TPU v7x, 32 devices: a whole 2x2x4 slice. The times are simulated.
32 devices in a mesh: dp: 4 (over z), expert: 8 (over y, x, core).
Axes of the slice: x: 2, y: 2, z: 4, core: 2. Of those that a mesh axis runs over, the one named last changes fastest.
Arguments:
- tokens: bfloat16 [2, 12288, 768], P(None, ('dp', 'expert')), may hold values from -6 to 6
- cotangent: bfloat16 [2, 12288, 768], P(None, ('dp', 'expert')), may hold values from -6 to 6
- token_ids: int32 [2, 12288], P(None, ('dp', 'expert')), may hold values from 0 to 8007, as said below
- hash_table: int32 [8008], replicated, may hold values from 0 to 7, as said below
- segment_ids: int32 [2, 12288], P(None, ('dp', 'expert')), may hold values from 0 to 1, as said below
- query_weight: bfloat16 [768, 768], replicated, may hold values from -0.21875 to 0.21875
- key_weight: bfloat16 [768, 768], replicated, may hold values from -0.21875 to 0.21875
- value_weight: bfloat16 [768, 768], replicated, may hold values from -0.21875 to 0.21875
- output_weight: bfloat16 [768, 768], replicated, may hold values from -2.5 to 2.5
- gain_attn: float32 [768], replicated, may hold values from 0.5 to 1.5
- gain_ffn: float32 [768], replicated, may hold values from 0.5 to 1.5
- expert_in: bfloat16 [8, 768, 3072], P('expert'), may hold values from -0.21875 to 0.21875
- expert_out: bfloat16 [8, 3072, 768], P('expert'), may hold values from -0.109375 to 0.109375
Outputs:
- block_out: bfloat16 [2, 12288, 768], P(None, ('dp', 'expert'))
- grad_tokens: bfloat16 [2, 12288, 768], P(None, ('dp', 'expert'))
- grad_query: float32 [768, 768], replicated
- grad_key: float32 [768, 768], replicated
- grad_value: float32 [768, 768], replicated
- grad_output: float32 [768, 768], replicated
- grad_gain_attn: float32 [768], replicated
- grad_gain_ffn: float32 [768], replicated
- grad_expert_in: float32 [8, 768, 3072], P('expert')
- grad_expert_out: float32 [8, 3072, 768], P('expert')
Inputs may be any that keep to these rules, and one draw needn't show every extreme that they name: hash_table sends 8008 // 8 or more ids to every expert. `token_ids`: in every micro-batch the 384 tokens of one device name any expert, through hash_table, at most 96 times; in every micro-batch one expert is named exactly 96 times by the tokens of every device. `segment_ids`: in each micro-batch a device's block holds either one sequence (all 0) or a sequence of 256 tokens (0) followed by one of the rest (1).
All inputs are finite; a program needn't handle non-finite values.
Results may differ from a plain program's by a relative error of at most 0.012.
Values may be sent and summed in bfloat16 or wider, within the bound.
No kernel may reach another device: no remote copies, remote signals or barrier semaphores. Data moves between devices by JAX's collectives and lax.ppermute only.
A program may use at most 192 MiB of HBM per device.

v0:
```python
import jax
import jax.numpy as jnp
from jax import lax
from jax.sharding import PartitionSpec as P

HEADS = 12
HEAD_DIM = 64


epsilon = 1e-05


def normalize(values, gain):
    return values * lax.rsqrt(jnp.mean(values * values, axis=-1, keepdims=True) + epsilon) * gain


def smooth_slope(values):
    sigmoid_part = jax.nn.sigmoid(values)
    return sigmoid_part * (1.0 + values * (1.0 - sigmoid_part))


def split_heads(matrix, head_count):
    return matrix.reshape(matrix.shape[0], head_count, -1).transpose(1, 0, 2)


def merge_heads(tensor):
    return tensor.transpose(1, 0, 2).reshape(tensor.shape[1], -1)


def masked_scores(query_heads, key_heads, allowed, score_scale):
    scores = (
        jnp.einsum("hqd,hkd->hqk", query_heads, key_heads, preferred_element_type=jnp.float32)
        * score_scale
    )
    return jnp.where(allowed[None], scores, -1e30)


def per_device(
    tokens,
    cotangent,
    token_ids,
    hash_table,
    segment_ids,
    query_weight,
    key_weight,
    value_weight,
    output_weight,
    gain_attn,
    gain_ffn,
    expert_in,
    expert_out,
):
    batches = tokens.shape[0]
    length = tokens.shape[1]
    model_width = tokens.shape[2]
    owners = lax.axis_size("expert")
    capacity = 2 * length // owners
    head_count = HEADS
    score_scale = HEAD_DIM ** (-0.5)
    weight_in = expert_in[0]
    weight_out = expert_out[0]
    position = jnp.arange(length, dtype=jnp.int32)
    float_type = jnp.float32
    half_type = jnp.bfloat16
    dense_total = (
        jnp.zeros(query_weight.shape, float_type),
        jnp.zeros(key_weight.shape, float_type),
        jnp.zeros(value_weight.shape, float_type),
        jnp.zeros(output_weight.shape, float_type),
        jnp.zeros(gain_attn.shape, float_type),
        jnp.zeros(gain_ffn.shape, float_type),
    )
    grad_in_sum = jnp.zeros(weight_in.shape, float_type)
    grad_out_sum = jnp.zeros(weight_out.shape, float_type)
    outputs = []
    grads_in = []
    for batch in range(batches):
        inputs_f = tokens[batch].astype(float_type)
        segments = segment_ids[batch]
        allowed = (position[:, None] >= position[None, :]) & (
            segments[:, None] == segments[None, :]
        )
        normed_attn = normalize(inputs_f, gain_attn).astype(half_type)
        query_heads = split_heads(
            jnp.dot(normed_attn, query_weight, preferred_element_type=float_type).astype(half_type),
            head_count,
        )
        key_heads = split_heads(
            jnp.dot(normed_attn, key_weight, preferred_element_type=float_type).astype(half_type),
            head_count,
        )
        value_heads = split_heads(
            jnp.dot(normed_attn, value_weight, preferred_element_type=float_type).astype(half_type),
            head_count,
        )
        scores = masked_scores(query_heads, key_heads, allowed, score_scale)
        row_peak = jnp.max(scores, axis=-1, keepdims=True)
        log_total = row_peak + jnp.log(jnp.sum(jnp.exp(scores - row_peak), axis=-1, keepdims=True))
        probs_low = jnp.exp(scores - log_total).astype(half_type)
        attended = merge_heads(
            jnp.einsum("hqk,hkd->hqd", probs_low, value_heads, preferred_element_type=float_type)
        ).astype(half_type)
        hidden = inputs_f + jnp.dot(attended, output_weight, preferred_element_type=float_type)
        routed = normalize(hidden, gain_ffn).astype(half_type)
        experts = jnp.take(hash_table, token_ids[batch])
        onehot = (experts[:, None] == jnp.arange(owners, dtype=jnp.int32)[None, :]).astype(
            jnp.int32
        )
        rank = jnp.sum((jnp.cumsum(onehot, axis=0, dtype=jnp.int32) - onehot) * onehot, axis=1)
        slot_index = experts * capacity + rank
        packed = jnp.zeros((owners * capacity, model_width), half_type).at[slot_index].set(routed)
        packed = packed.reshape(owners, capacity, model_width)
        received = lax.all_to_all(
            packed, "expert", split_axis=0, concat_axis=0, tiled=True
        ).reshape(owners * capacity, model_width)
        pre_active = jnp.dot(received, weight_in, preferred_element_type=float_type)
        active = jax.nn.silu(pre_active).astype(half_type)
        produced = jnp.dot(active, weight_out, preferred_element_type=float_type).astype(half_type)
        returned = lax.all_to_all(
            produced.reshape(owners, capacity, model_width),
            "expert",
            split_axis=0,
            concat_axis=0,
            tiled=True,
        )
        returned = returned.reshape(owners * capacity, model_width)
        block_out = hidden + jnp.take(returned, slot_index, axis=0).astype(float_type)
        outputs.append(block_out.astype(half_type))
        grad_block = cotangent[batch].astype(float_type)
        grad_result = grad_block.astype(half_type)
        grad_packed = (
            jnp.zeros((owners * capacity, model_width), half_type).at[slot_index].set(grad_result)
        )
        grad_packed = grad_packed.reshape(owners, capacity, model_width)
        grad_recv = lax.all_to_all(grad_packed, "expert", split_axis=0, concat_axis=0, tiled=True)
        grad_recv = grad_recv.reshape(owners * capacity, model_width)
        slope = smooth_slope(pre_active)
        grad_out_sum = grad_out_sum + jnp.dot(
            active.T, grad_recv, preferred_element_type=float_type
        )
        grad_active = jnp.dot(grad_recv, weight_out.T, preferred_element_type=float_type)
        grad_pre = (grad_active * slope).astype(half_type)
        grad_in_sum = grad_in_sum + jnp.dot(received.T, grad_pre, preferred_element_type=float_type)
        grad_rows = jnp.dot(grad_pre, weight_in.T, preferred_element_type=float_type).astype(
            half_type
        )
        grad_back = lax.all_to_all(
            grad_rows.reshape(owners, capacity, model_width),
            "expert",
            split_axis=0,
            concat_axis=0,
            tiled=True,
        )
        grad_routed = jnp.take(
            grad_back.reshape(owners * capacity, model_width), slot_index, axis=0
        ).astype(float_type)
        ignored_ffn, pull_ffn = jax.vjp(normalize, hidden, gain_ffn)
        grad_from_ffn, grad_gain_two = pull_ffn(grad_routed)
        grad_hidden = grad_block + grad_from_ffn
        grad_attn = grad_hidden.astype(half_type)
        grad_output_term = jnp.dot(attended.T, grad_attn, preferred_element_type=float_type)
        grad_mixed = split_heads(
            jnp.dot(grad_attn, output_weight.T, preferred_element_type=float_type).astype(
                half_type
            ),
            head_count,
        )
        scores_again = masked_scores(query_heads, key_heads, allowed, score_scale)
        probs = jnp.exp(scores_again - log_total)
        probs_again = probs.astype(half_type)
        grad_values = jnp.einsum(
            "hqk,hqd->hkd", probs_again, grad_mixed, preferred_element_type=float_type
        ).astype(half_type)
        grad_probs = jnp.einsum(
            "hqd,hkd->hqk", grad_mixed, value_heads, preferred_element_type=float_type
        )
        shared = jnp.sum(probs * grad_probs, axis=-1, keepdims=True)
        grad_scores = (probs * (grad_probs - shared)).astype(half_type)
        grad_queries = (
            jnp.einsum("hqk,hkd->hqd", grad_scores, key_heads, preferred_element_type=float_type)
            * score_scale
        ).astype(half_type)
        grad_keys = (
            jnp.einsum("hqk,hqd->hkd", grad_scores, query_heads, preferred_element_type=float_type)
            * score_scale
        ).astype(half_type)
        grad_queries = merge_heads(grad_queries)
        grad_keys = merge_heads(grad_keys)
        grad_values = merge_heads(grad_values)
        grad_query_term = jnp.dot(normed_attn.T, grad_queries, preferred_element_type=float_type)
        grad_key_term = jnp.dot(normed_attn.T, grad_keys, preferred_element_type=float_type)
        grad_value_term = jnp.dot(normed_attn.T, grad_values, preferred_element_type=float_type)
        grad_normed = (
            jnp.dot(grad_queries, query_weight.T, preferred_element_type=float_type)
            + jnp.dot(grad_keys, key_weight.T, preferred_element_type=float_type)
            + jnp.dot(grad_values, value_weight.T, preferred_element_type=float_type)
        )
        ignored_attn, pull_attn = jax.vjp(normalize, inputs_f, gain_attn)
        grad_from_attn, grad_gain_one = pull_attn(grad_normed)
        grads_in.append((grad_hidden + grad_from_attn).astype(half_type))
        terms = (
            grad_query_term,
            grad_key_term,
            grad_value_term,
            grad_output_term,
            grad_gain_one,
            grad_gain_two,
        )
        dense_total = tuple((total + term for total, term in zip(dense_total, terms)))
    dense_total = lax.psum(
        (
            dense_total[0],
            dense_total[1],
            dense_total[2],
            dense_total[3],
            dense_total[4],
            dense_total[5],
        ),
        ("dp", "expert"),
    )
    expert_in_sum, expert_out_sum = (
        lax.psum(grad_in_sum.astype(jnp.bfloat16), "dp").astype(jnp.float32),
        lax.psum(grad_out_sum.astype(jnp.bfloat16), "dp").astype(jnp.float32),
    )
    return (
        jnp.stack(outputs),
        jnp.stack(grads_in),
        dense_total[0],
        dense_total[1],
        dense_total[2],
        dense_total[3],
        dense_total[4],
        dense_total[5],
        expert_in_sum[None],
        expert_out_sum[None],
    )


def solution(mesh):
    placed = (
        P(None, ("dp", "expert"), None),
        P(None, ("dp", "expert"), None),
        P(None, ("dp", "expert")),
        P(),
        P(None, ("dp", "expert")),
        P(),
        P(),
        P(),
        P(),
        P(),
        P(),
        P("expert", None, None),
        P("expert", None, None),
    )
    return jax.shard_map(
        per_device,
        mesh=mesh,
        in_specs=placed,
        out_specs=(
            P(None, ("dp", "expert"), None),
            P(None, ("dp", "expert"), None),
            P(),
            P(),
            P(),
            P(),
            P(),
            P(),
            P("expert", None, None),
            P("expert", None, None),
        ),
        check_vma=False,
    )
```

profile of v0, /device:TPU:0, one launch (start us, length us, event | category | flops | bytes accessed | tf_op | source)
XLA Modules:
  0.0 789.7 jit_solution(1991907835853382940)
XLA Ops:
  36.2 3.9 scatter_custom_fusion
  40.1 5.7 all-to-all-start
  63.0 5.8 convolution_convert_fusion
  76.1 4.3 all-to-all-start.2
  88.1 9.2 %all-to-all-done.2 = bf16[8,96,768]{2,1,0:T(8,128)(2,1)S(1)} async-done(((bf16[8,96,768]{2,1,0:T(8,128)(2,1)}), bf16[8,96,768]{2,1,0:T(8,128)(2,1)S(1)}, u32[]{:S(2)}, u32[]{:S(2)}) %all-to-all-start.2) | async-done | bytes 1179680 | tf_op jit(solution)/shard_map/all_to_all | solution.py:113
  100.9 12.6 %multiply_convert_fusion.3 = (bf16[768,3072]{1,0:T(8,128)(2,1)}, f32[768,3072]{1,0:T(8,128)}) fusion(bf16[768,768]{1,0:T(8,128)(2,1)} %bitcast.13, bf16[1,768,3072]{2,1,0:T(8,128)(2,1)} %param.28), kind=kOutput, calls=%fused_computation.16 | convolution fusion | flops 3635675136 | bytes 20054016 | tf_op jit(solution)/shard_map/dot_general | solution.py:116
  113.5 8.5 %fusion.12 = f32[768,3072]{1,0:T(8,128)} fusion(bf16[768,768]{1,0:T(8,128)(2,1)S(1)} %bitcast.311, bf16[1,768,3072]{2,1,0:T(8,128)(2,1)} %param.28), kind=kOutput, calls=%fused_computation.40 | convolution fusion | flops 3623878656 | bytes 15335424 | tf_op jit(solution)/shard_map/dot_general | solution.py:116
  122.0 4.1 all-to-all-start.6
  126.1 8.8 %multiply_convert_fusion.1 = bf16[768,3072]{1,0:T(8,128)(2,1)S(1)} fusion(f32[768,3072]{1,0:T(8,128)} %get-tuple-element.57, bf16[768,768]{1,0:T(8,128)(2,1)S(1)} %bitcast.314, bf16[1,3072,768]{2,1,0:T(8,128)(2,1)} %param.29), kind=kOutput, calls=%fused_computation.13 | convolution fusion | flops 3645112320 | bytes 20054016 | tf_op jit(solution)/shard_map/dot_general | solution.py:141
  135.0 10.2 %fusion.145 = f32[3072,768]{1,0:T(8,128)} fusion(bf16[768,3072]{1,0:T(8,128)(2,1)} %get-tuple-element.56, bf16[768,768]{1,0:T(8,128)(2,1)S(1)} %bitcast.315), kind=kOutput, calls=%fused_computation.230 | convolution fusion | flops 3623878656 | bytes 15335424 | tf_op jit(solution)/shard_map/dot_general | solution.py:138
  145.2 7.2 fusion.20
  152.4 4.4 all-to-all-start.5
  156.9 8.9 %multiply_convert_fusion = bf16[768,3072]{1,0:T(8,128)(2,1)S(1)} fusion(f32[768,3072]{1,0:T(8,128)} %fusion.12, bf16[768,768]{1,0:T(8,128)(2,1)S(1)} %bitcast.316, bf16[1,3072,768]{2,1,0:T(8,128)(2,1)} %param.29), kind=kOutput, calls=%fused_computation.12 | convolution fusion | flops 3645112320 | bytes 20054016 | tf_op jit(solution)/shard_map/dot_general | solution.py:141
  165.8 15.0 %fusion.17 = bf16[1,3072,768]{2,1,0:T(8,128)(2,1)} fusion(f32[3072,768]{1,0:T(8,128)} %fusion.145, bf16[768,768]{1,0:T(8,128)(2,1)S(1)} %bitcast.317, f32[768,3072]{1,0:T(8,128)} %fusion.12), kind=kOutput, calls=%fused_computation.45 | convolution fusion | flops 3640393728 | bytes 24772608 | tf_op jit(solution)/shard_map/dot_general | solution.py:138
  180.9 4.9 fusion.23
  185.7 4.6 all-to-all-start.7
  190.4 11.1 %fusion.29 = bf16[768,768]{1,0:T(8,128)(2,1)} fusion(bf16[1,3072,768]{2,1,0:T(8,128)(2,1)} %param.29, f32[768,3072]{1,0:T(8,128)} %fusion.12), kind=kOutput, calls=%fused_computation.59 | convolution fusion | flops 3636264960 | bytes 15335424 | tf_op jit(solution)/shard_map/dot_general | solution.py:118
  201.4 5.7 all-to-all-done.7
  207.2 4.3 all-to-all-start.3
  211.4 10.3 %fusion.144 = f32[768,3072]{1,0:T(8,128)} fusion(bf16[768,768]{1,0:T(8,128)(2,1)} %bitcast.13, bf16[768,3072]{1,0:T(8,128)(2,1)} %copy-done.26), kind=kOutput, calls=%fused_computation.229 | convolution fusion | flops 3623878656 | bytes 15335424 | tf_op jit(solution)/shard_map/dot_general | solution.py:143
  221.8 8.6 %fusion.26 = bf16[768,768]{1,0:T(8,128)(2,1)} fusion(bf16[768,3072]{1,0:T(8,128)(2,1)} %get-tuple-element.56, bf16[1,3072,768]{2,1,0:T(8,128)(2,1)} %param.29), kind=kOutput, calls=%fused_computation.58 | convolution fusion | flops 3624468480 | bytes 10616832 | tf_op jit(solution)/shard_map/dot_general | solution.py:118
  230.4 4.3 all-to-all-start.1
  234.9 11.5 %fusion.16 = bf16[1,768,3072]{2,1,0:T(8,128)(2,1)} fusion(f32[768,3072]{1,0:T(8,128)} %fusion.144, bf16[768,768]{1,0:T(8,128)(2,1)} %bitcast.312, bf16[768,3072]{1,0:T(8,128)(2,1)} %copy-done.92), kind=kOutput, calls=%fused_computation.44 | convolution fusion | flops 3628597248 | bytes 20054016 | tf_op jit(solution)/shard_map/dot_general | solution.py:143
  249.7 4.4 gather_fusion.3
  260.6 4.4 gather_fusion.1
  265.0 4.2 fusion.70
  277.9 5.6 multiply_reduce_fusion.1
  325.5 46.7 %all-reduce = (f32[768]{0:T(1024)}, f32[768]{0:T(1024)}) all-reduce(f32[768]{0:T(1024)} %add.207, f32[768]{0:T(1024)} %add.208), channel_id=1, replica_groups=mesh['dp'=4,'expert'=8] {'dp','expert'}, use_global_device_ids=true, to_apply=%region_30.33 | all-reduce | flops 1536 | bytes 12288 | tf_op jit(solution)/shard_map/psum | solution.py:210
  378.5 196.6 %all-reduce.8.cloned.1.call-done = (bf16[1,768,3072]{2,1,0:T(8,128)(2,1)}, bf16[1,3072,768]{2,1,0:T(8,128)(2,1)}) async-done(((bf16[1,768,3072]{2,1,0:T(8,128)(2,1)}, bf16[1,3072,768]{2,1,0:T(8,128)(2,1)}), (bf16[1,768,3072]{2,1,0:T(8,128)(2,1)}, bf16[1,3072,768]{2,1,0:T(8,128)(2,1)})) %all-reduce.8.cloned.1.call-update) | async-done | bytes 9437200 | tf_op jit(solution)/shard_map/psum | solution.py:222
  575.1 7.5 broadcast_in_dim.117
  582.6 4.9 broadcast_in_dim.119
  587.5 185.4 %all-reduce.6.cloned.1.call-done = (f32[768,768]{1,0:T(8,128)}, f32[768,768]{1,0:T(8,128)}, f32[768,768]{1,0:T(8,128)}, f32[768,768]{1,0:T(8,128)}) async-done(((f32[768,768]{1,0:T(8,128)}, f32[768,768]{1,0:T(8,128)}, f32[768,768]{1,0:T(8,128)}, f32[768,768]{1,0:T(8,128)}), (f32[768,768]{1,0:T(8,128)}, f32[768,768]{1,0:T(8,128)}, f32[768,768]{1,0:T(8,128)}, ...) | async-done | bytes 9437200 | tf_op jit(solution)/shard_map/psum | solution.py:210
  (309 shorter events, 140.4 us)
Async XLA Ops:
  8.9 36.9 %copy-start.79 = (f32[384]{0:T(512)}, f32[384]{0:T(512)S(1)}, u32[]{:S(2)}) copy-start(f32[384]{0:T(512)S(1)} %get-tuple-element.23) | copy-start | bytes 4612
  9.5 8.2 %copy-start.69 = (f32[384]{0:T(512)}, f32[384]{0:T(512)S(1)}, u32[]{:S(2)}) copy-start(f32[384]{0:T(512)S(1)} %fusion.115) | copy-start | bytes 4612
  17.7 4.4 copy-start.11
  31.1 5.1 copy-start.67
  31.7 8.4 %copy-start.73 = (f32[384]{0:T(512)}, f32[384]{0:T(512)S(1)}, u32[]{:S(2)}) copy-start(f32[384]{0:T(512)S(1)} %fusion.116) | copy-start | bytes 4612
  40.1 36.0 %all-to-all-start = ((bf16[8,96,768]{2,1,0:T(8,128)(2,1)}), bf16[8,96,768]{2,1,0:T(8,128)(2,1)}, u32[]{:S(2)}, u32[]{:S(2)}) async-start(bf16[8,96,768]{2,1,0:T(8,128)(2,1)} %bitcast.300), calls=%async_computation | async-start | bytes 2359296 | tf_op jit(solution)/shard_map/all_to_all | solution.py:113
  51.3 11.7 %copy-start.40 = (pred[384,384]{0,1:T(8,128)(4,1)}, pred[384,384]{0,1:T(8,128)(4,1)S(1)}, u32[]{:S(2)}) copy-start(pred[384,384]{0,1:T(8,128)(4,1)S(1)} %fusion.96) | copy-start | bytes 442372
  52.8 4.7 copy-start.15
  60.4 8.4 %copy-start.63 = (f32[12,384]{1,0:T(8,128)}, f32[12,384]{1,0:T(8,128)S(1)}, u32[]{:S(2)}) copy-start(f32[12,384]{1,0:T(8,128)S(1)} %log_add_fusion) | copy-start | bytes 55300
  76.1 4.4 copy-start.27
  76.1 21.2 %all-to-all-start.2 = ((bf16[8,96,768]{2,1,0:T(8,128)(2,1)}), bf16[8,96,768]{2,1,0:T(8,128)(2,1)S(1)}, u32[]{:S(2)}, u32[]{:S(2)}) async-start(bf16[8,96,768]{2,1,0:T(8,128)(2,1)} %bitcast.31), calls=%async_computation.2 | async-start | bytes 2359296 | tf_op jit(solution)/shard_map/all_to_all | solution.py:113
  97.3 16.2 %copy-start.54 = (bf16[8,96,768]{2,1,0:T(8,128)(2,1)}, bf16[8,96,768]{2,1,0:T(8,128)(2,1)S(1)}, u32[]{:S(2)}) copy-start(bf16[8,96,768]{2,1,0:T(8,128)(2,1)S(1)} %all-to-all-done.2) | copy-start | bytes 3538948
  97.3 24.7 %all-to-all-start.4 = ((bf16[8,96,768]{2,1,0:T(8,128)(2,1)}), bf16[8,96,768]{2,1,0:T(8,128)(2,1)S(1)}, u32[]{:S(2)}, u32[]{:S(2)}) async-start(bf16[8,96,768]{2,1,0:T(8,128)(2,1)} %bitcast.37), calls=%async_computation.4 | async-start | bytes 2359296 | tf_op jit(solution)/shard_map/all_to_all | solution.py:135
  122.0 30.4 %all-to-all-start.6 = ((bf16[8,96,768]{2,1,0:T(8,128)(2,1)}), bf16[8,96,768]{2,1,0:T(8,128)(2,1)S(1)}, u32[]{:S(2)}, u32[]{:S(2)}) async-start(bf16[8,96,768]{2,1,0:T(8,128)(2,1)} %bitcast.55), calls=%async_computation.6 | async-start | bytes 2359296 | tf_op jit(solution)/shard_map/all_to_all | solution.py:135
  134.9 10.3 %copy-start.26 = (bf16[768,3072]{1,0:T(8,128)(2,1)}, bf16[768,3072]{1,0:T(8,128)(2,1)S(1)}, u32[]{:S(2)}) copy-start(bf16[768,3072]{1,0:T(8,128)(2,1)S(1)} %multiply_convert_fusion.1) | copy-start | bytes 14155780
  152.4 33.3 %all-to-all-start.5 = ((bf16[8,96,768]{2,1,0:T(8,128)(2,1)}), bf16[8,96,768]{2,1,0:T(8,128)(2,1)S(1)}, u32[]{:S(2)}, u32[]{:S(2)}) async-start(bf16[8,96,768]{2,1,0:T(8,128)(2,1)} %bitcast.319), calls=%async_computation.5 | async-start | bytes 2359296 | tf_op jit(solution)/shard_map/all_to_all | solution.py:147
  156.8 24.0 %slice-start.4 = ((s8[4718592]{0:T(1024)(128)(4,1)}), s8[4194304]{0:T(1024)(128)(4,1)S(1)}, s32[]{:S(2)}) async-start(s8[4718592]{0:T(1024)(128)(4,1)} %bitcast.331), calls=%async_computation.14 | async-start | bytes 8388608
  165.8 15.0 %copy-start.92 = (bf16[768,3072]{1,0:T(8,128)(2,1)}, bf16[768,3072]{1,0:T(8,128)(2,1)S(1)}, u32[]{:S(2)}) copy-start(bf16[768,3072]{1,0:T(8,128)(2,1)S(1)} %multiply_convert_fusion) | copy-start | bytes 14155780
  165.8 15.0 %slice-start.5 = ((s8[4718592]{0:T(1024)(128)(4,1)}), s8[524288]{0:T(1024)(128)(4,1)S(1)}, s32[]{:S(2)}) async-start(s8[4718592]{0:T(1024)(128)(4,1)} %bitcast.331), calls=%async_computation.15 | async-start | bytes 1048576
  185.7 21.4 %all-to-all-start.7 = ((bf16[8,96,768]{2,1,0:T(8,128)(2,1)}), bf16[8,96,768]{2,1,0:T(8,128)(2,1)S(1)}, u32[]{:S(2)}, u32[]{:S(2)}) async-start(bf16[8,96,768]{2,1,0:T(8,128)(2,1)} %bitcast.320), calls=%async_computation.7 | async-start | bytes 2359296 | tf_op jit(solution)/shard_map/all_to_all | solution.py:147
  207.2 23.2 %all-to-all-start.3 = ((bf16[8,96,768]{2,1,0:T(8,128)(2,1)}), bf16[8,96,768]{2,1,0:T(8,128)(2,1)}, u32[]{:S(2)}, u32[]{:S(2)}) async-start(bf16[8,96,768]{2,1,0:T(8,128)(2,1)} %bitcast.318), calls=%async_computation.3 | async-start | bytes 2359296 | tf_op jit(solution)/shard_map/all_to_all | solution.py:119
  230.4 30.2 %all-to-all-start.1 = ((bf16[8,96,768]{2,1,0:T(8,128)(2,1)}), bf16[8,96,768]{2,1,0:T(8,128)(2,1)}, u32[]{:S(2)}, u32[]{:S(2)}) async-start(bf16[8,96,768]{2,1,0:T(8,128)(2,1)} %bitcast.313), calls=%async_computation.1 | async-start | bytes 2359296 | tf_op jit(solution)/shard_map/all_to_all | solution.py:119
  234.6 340.4 %all-reduce.8.cloned.1.call-start = ((), (), s32[]{:S(2)}) async-start(), calls=%async_computation.9 | async-start | bytes 18874368 | tf_op jit(solution)/shard_map/psum | solution.py:222
  246.4 526.4 %all-reduce.6.cloned.1.call-start = ((), (), s32[]{:S(2)}) async-start(), calls=%async_computation.8 | async-start | bytes 18874368 | tf_op jit(solution)/shard_map/psum | solution.py:210
  249.7 4.5 copy-start.81
  260.6 4.4 copy-start.88
  277.9 5.7 slice-start
  277.9 5.7 slice-start.1
  288.2 7.2 slice-start.2
  291.0 4.5 slice-start.3
  321.8 53.0 %copy-start.80 = (f32[384]{0:T(512)S(1)}, f32[384]{0:T(512)}, u32[]{:S(2)}) copy-start(f32[384]{0:T(512)} %copy-done.79) | copy-start | bytes 4612
  575.1 7.5 copy-start.25
  (77 other events, 164.5 us)
Sparse Core Ops, SparseCore 0:
  246.5 328.4 all-reduce.7
  581.9 190.9 all-reduce.5
where the time goes:
time: 799 us; the launch traced here: 790 us
  waiting for transfers between devices  397 us (50%)
  matrix products  184 us (23%)
  local copies, waits for them, and re-layouts  61.3 us (8%)
  other arithmetic  49.6 us (6%)
  blocking collectives  46.7 us (6%)
  starting transfers between devices  35.6 us (4%)
  between operations  15.4 us (2%)
    psum x1, waiting for transfers between devices, per_device(): lax.psum(grad_in_sum.astype(jnp.bfloat16), 'dp').astype(jnp.float32)  197 us
    psum x1, waiting for transfers between devices, per_device(): lax.psum((dense_total[0], dense_total[1], dense_total[2], dense_total[3],...  185 us
    psum x1, blocking collectives, per_device(): lax.psum((dense_total[0], dense_total[1], dense_total[2], dense_total[3],...  46.7 us
    dot_general x2, matrix products, per_device(): jnp.dot(active.T, grad_recv, preferred_element_type=float_type)  25.3 us
    dot_general x2, matrix products, per_device(): jnp.dot(received.T, grad_pre, preferred_element_type=float_type)  21.9 us
    dot_general x2, matrix products, per_device(): pre_active = jnp.dot(received, weight_in, preferred_element_type=float_type)  21.1 us
    unnamed x202, local copies, waits for them, and re-layouts  20.3 us
    dot_general x2, matrix products, per_device(): jnp.dot(active, weight_out, preferred_element_type=float_type)  19.7 us
  transfers between devices with their start and end apart: 10, of which 4 were waited for; matrix products, arithmetic and copies ran while one was open for 31% of the time, Pallas kernels for 0%

commit v1 on v0

v1 whole, which is shorter than its diff:
```python
import functools

import jax
import jax.numpy as jnp
from jax import lax
from jax.experimental import pallas as pl
from jax.experimental.pallas import tpu as pltpu
from jax.sharding import PartitionSpec as P

HEADS = 12
HEAD_DIM = 64
EPS = 1e-05
SCALE = HEAD_DIM ** (-0.5)
PAIR = 2 * HEAD_DIM
F32 = jnp.float32
BF16 = jnp.bfloat16
VMEM_LIMIT = 56 * 1024 * 1024


def dot(a, b, ca=1, cb=0):
    return lax.dot_general(a, b, (((ca,), (cb,)), ((), ())), preferred_element_type=F32)


def params(n):
    return pltpu.CompilerParams(
        dimension_semantics=("arbitrary",) * n, vmem_limit_bytes=VMEM_LIMIT
    )


def full(*shape):
    return pl.BlockSpec(shape, lambda *_: (0,) * len(shape))


ANY = pl.BlockSpec(memory_space=pl.ANY)


def iota(shape, axis):
    return lax.broadcasted_iota(jnp.int32, shape, axis)


def to_column(row):
    n = row.shape[1]
    eye = iota((n, n), 0) == iota((n, n), 1)
    return jnp.sum(jnp.where(eye, row, 0), axis=1, keepdims=True)


def route_kernel(m, owners, cap, ids_ref, table_ref, cot_ref, slot_ref, pack_ref):
    n = ids_ref.shape[1]
    ids = ids_ref[pl.ds(m, 1), :]
    rows = table_ref.shape[0]
    pick = (iota((rows, n), 0) == (ids >> 7)).astype(BF16)
    values = dot(table_ref[...].astype(BF16), pick, 0, 0)
    lane = ids & 127
    expert = jnp.sum(jnp.where(iota((128, n), 0) == lane, values, 0.0), axis=0, keepdims=True)
    kinds = -(-owners // 16) * 16
    named = iota((kinds, n), 0).astype(F32) == expert
    before = (iota((n, n), 0) < iota((n, n), 1)).astype(BF16)
    counts = dot(named.astype(BF16), before)
    rank = jnp.sum(jnp.where(named, counts, 0.0), axis=0, keepdims=True)
    slot = (expert * cap + rank).astype(jnp.int32)
    slot_ref[...] = slot
    places = (iota((owners * cap, n), 0) == slot).astype(BF16)
    pack_ref[...] = dot(places, cot_ref[0]).astype(BF16)


def route(m, ids, table, cot, owners, cap):
    micro, n = ids.shape
    width = cot.shape[2]
    rows = table.shape[0]
    return pl.pallas_call(
        functools.partial(route_kernel, m, owners, cap),
        grid=(1,),
        in_specs=[
            full(micro, n), full(rows, 128), pl.BlockSpec((1, n, width), lambda i: (m, 0, 0)),
        ],
        out_specs=[full(1, n), full(owners * cap, width)],
        out_shape=[
            jax.ShapeDtypeStruct((1, n), jnp.int32),
            jax.ShapeDtypeStruct((owners * cap, width), BF16),
        ],
        compiler_params=params(1),
    )(ids, table, cot)


def bias_of(seg):
    n = seg.shape[1]
    key, query = iota((n, n), 0), iota((n, n), 1)
    seen = (key <= query) & (to_column(seg) == seg)
    return jnp.where(seen, 0.0, -1e30)


def forward_kernel(
    m, slot_ref, seg_ref, tok_ref, wq_ref, wk_ref, wv_ref, wo_ref, ga_ref, gf_ref, dep_ref,
    normed_ref, q_ref, k_ref, v_ref, lse_ref, mixed_ref, hidden_ref, pack_ref, bias_ref,
):
    x = tok_ref[0].astype(F32)
    n = x.shape[0]
    r = lax.rsqrt(jnp.mean(x * x, axis=1, keepdims=True) + EPS)
    normed = (x * r * ga_ref[...]).astype(BF16)
    normed_ref[...] = normed
    q_ref[...] = (dot(normed, wq_ref[...]).astype(BF16) * SCALE).astype(BF16)
    k_ref[...] = dot(normed, wk_ref[...]).astype(BF16)
    v_ref[...] = dot(normed, wv_ref[...]).astype(BF16)
    bias_ref[...] = bias_of(seg_ref[pl.ds(m, 1), :])
    low = iota((n, PAIR), 1) < HEAD_DIM

    def pair(p, carry):
        cols = pl.ds(pl.multiple_of(p * PAIR, PAIR), PAIR)
        q, k, v = q_ref[:, cols], k_ref[:, cols], v_ref[:, cols]
        parts = []
        for h in range(2):
            mine = low if h == 0 else ~low
            s = dot(k, jnp.where(mine, q, 0), 1, 1) + bias_ref[...]
            top = jnp.max(s, axis=0, keepdims=True)
            e = jnp.exp(s - top)
            total = jnp.sum(e, axis=0, keepdims=True)
            lse_ref[pl.ds(2 * p + h, 1), :] = top + jnp.log(total)
            probs = (e * (1.0 / total)).astype(BF16)
            parts.append(dot(probs, v, 0, 0))
        mixed_ref[:, cols] = jnp.where(low, parts[0], parts[1]).astype(BF16)
        return carry

    lax.fori_loop(0, HEADS // 2, pair, 0)
    hidden = x + dot(mixed_ref[...], wo_ref[...])
    hidden_ref[...] = hidden
    r = lax.rsqrt(jnp.mean(hidden * hidden, axis=1, keepdims=True) + EPS)
    routed = (hidden * r * gf_ref[...]).astype(BF16)
    places = (iota((pack_ref.shape[0], n), 0) == slot_ref[...]).astype(BF16)
    pack_ref[...] = dot(places, routed).astype(BF16)


def forward(m, slot, seg, tokens, wq, wk, wv, wo, ga, gf, slots, dep):
    _, n, d = tokens.shape
    shapes = [
        ((n, d), BF16), ((n, d), BF16), ((n, d), BF16), ((n, d), BF16), ((16, n), F32),
        ((n, d), BF16), ((n, d), F32), ((slots, d), BF16),
    ]
    return pl.pallas_call(
        functools.partial(forward_kernel, m),
        grid=(1,),
        in_specs=[
            full(1, n), full(*seg.shape), pl.BlockSpec((1, n, d), lambda i: (m, 0, 0)),
            full(d, d), full(d, d), full(d, d), full(d, d), full(1, d), full(1, d), ANY,
        ],
        out_specs=[full(*s) for s, _ in shapes],
        out_shape=[jax.ShapeDtypeStruct(s, t) for s, t in shapes],
        scratch_shapes=[pltpu.VMEM((n, n), F32)],
        compiler_params=params(1),
    )(slot, seg, tokens, wq, wk, wv, wo, ga, gf, dep)


BLOCK = 256


def expert_kernel(rx0_ref, rx1_ref, g0_ref, g1_ref, win_ref, wout_ref, *rest):
    chunk_ref, act_ref, gpre_ref = rest[-3:]
    win, wout = win_ref[0], wout_ref[0]
    f = win.shape[1]
    rows = rx0_ref.shape[0]
    gout, gin = None, None
    for m, (x_ref, g_ref) in enumerate(((rx0_ref, g0_ref), (rx1_ref, g1_ref))):
        x, g = x_ref[...], g_ref[...]
        pre = dot(x, win)
        sig = jax.nn.sigmoid(pre)
        act = (pre * sig).astype(BF16)
        slope = sig * (1.0 + pre * (1.0 - sig))
        gpre = (dot(g, wout, 1, 1) * slope).astype(BF16)
        act_ref[pl.ds(m * rows, rows), :] = act
        gpre_ref[pl.ds(m * rows, rows), :] = gpre
        a, b = dot(act, g, 0, 0), dot(gpre, x, 0, 0)
        gout, gin = (a, b) if m == 0 else (gout + a, gin + b)
    chunk_ref[pl.ds(0, f), :] = gout.astype(BF16)
    chunk_ref[pl.ds(f, f), :] = gin.astype(BF16)


def expert(c, units, rx, g, win, wout, held, dep):
    rows, d = rx[0].shape
    ff = win.shape[2]
    f = BLOCK
    extra = ([] if held is None else list(held)) + [dep]
    alias = {} if held is None else {6: 1, 7: 2}
    return pl.pallas_call(
        expert_kernel,
        grid=(units,),
        in_specs=[full(rows, d)] * 4
        + [
            pl.BlockSpec((1, d, f), lambda i: (0, 0, c + i)),
            pl.BlockSpec((1, f, d), lambda i: (0, c + i, 0)),
        ]
        + [ANY] * len(extra),
        out_specs=[
            pl.BlockSpec((2 * f, d), lambda i: (i, 0)),
            pl.BlockSpec((2 * rows, f), lambda i: (0, c + i)),
            pl.BlockSpec((2 * rows, f), lambda i: (0, c + i)),
        ],
        out_shape=[
            jax.ShapeDtypeStruct((units * 2 * f, d), BF16),
            jax.ShapeDtypeStruct((2 * rows, ff), BF16),
            jax.ShapeDtypeStruct((2 * rows, ff), BF16),
        ],
        input_output_aliases=alias,
        compiler_params=params(1),
    )(*rx, *g, win, wout, *extra)


def rows_kernel(side, a_ref, w_ref, dep_ref, o_ref):
    o_ref[...] = dot(a_ref[...], w_ref[0], 1, side).astype(BF16)


def back_rows(m, a, w, side, dep, blk=384):
    ff = a.shape[1]
    rows = a.shape[0] // 2
    d = w.shape[1 + (1 - side)]
    steps = rows // blk
    return pl.pallas_call(
        functools.partial(rows_kernel, side),
        grid=(steps,),
        in_specs=[pl.BlockSpec((blk, ff), lambda i: (m * steps + i, 0)), full(*w.shape), ANY],
        out_specs=pl.BlockSpec((blk, d), lambda i: (i, 0)),
        out_shape=jax.ShapeDtypeStruct((rows, d), BF16),
        compiler_params=params(1),
    )(a, w, dep)


def backward_kernel(
    m, slot_ref, seg_ref, tok_ref, cot_ref, back_ref, normed_ref, q_ref, k_ref, v_ref, lse_ref,
    hidden_ref, wq_ref, wk_ref, wv_ref, wo_ref, ga_ref, gf_ref, *rest,
):
    gtok_ref, gattn_ref, gq_ref, gk_ref, gv_ref, gain_ref, bias_ref, gm_ref, gh_ref = rest[-9:]
    n, d = normed_ref.shape
    slots = back_ref.shape[0]
    places = (iota((n, slots), 1) == to_column(slot_ref[...])).astype(BF16)
    grad_routed = dot(places, back_ref[...])
    hidden = hidden_ref[...]
    r = lax.rsqrt(jnp.mean(hidden * hidden, axis=1, keepdims=True) + EPS)
    unit = hidden * r
    g = grad_routed * gf_ref[...]
    grad_hidden = cot_ref[0].astype(F32) + r * (
        g - unit * jnp.mean(g * unit, axis=1, keepdims=True)
    )
    gh_ref[...] = grad_hidden
    gain_ref[pl.ds(1, 1), :] = jnp.sum(grad_routed * unit, axis=0, keepdims=True)
    grad_attn = grad_hidden.astype(BF16)
    gattn_ref[...] = grad_attn
    gm_ref[...] = dot(grad_attn, wo_ref[...], 1, 1).astype(BF16)
    bias_ref[...] = bias_of(seg_ref[pl.ds(m, 1), :])
    low = iota((n, PAIR), 1) < HEAD_DIM

    def pair(p, carry):
        cols = pl.ds(pl.multiple_of(p * PAIR, PAIR), PAIR)
        q, k, v, gm = q_ref[:, cols], k_ref[:, cols], v_ref[:, cols], gm_ref[:, cols]
        gqs, gks, gvs = [], [], []
        for h in range(2):
            mine = low if h == 0 else ~low
            s = dot(k, jnp.where(mine, q, 0), 1, 1) + bias_ref[...]
            probs = jnp.exp(s - lse_ref[pl.ds(2 * p + h, 1), :])
            gvs.append(dot(probs.astype(BF16), gm))
            gp = dot(v, jnp.where(mine, gm, 0), 1, 1)
            shared = jnp.sum(probs * gp, axis=0, keepdims=True)
            gs = (probs * (gp - shared)).astype(BF16)
            gks.append(dot(gs, q))
            gqs.append(dot(gs, k, 0, 0))
        gq_ref[:, cols] = (jnp.where(low, gqs[0], gqs[1]) * SCALE).astype(BF16)
        gk_ref[:, cols] = jnp.where(low, gks[0], gks[1]).astype(BF16)
        gv_ref[:, cols] = jnp.where(low, gvs[0], gvs[1]).astype(BF16)
        return carry

    lax.fori_loop(0, HEADS // 2, pair, 0)
    grad_normed = (
        dot(gq_ref[...], wq_ref[...], 1, 1)
        + dot(gk_ref[...], wk_ref[...], 1, 1)
        + dot(gv_ref[...], wv_ref[...], 1, 1)
    )
    x = tok_ref[0].astype(F32)
    r = lax.rsqrt(jnp.mean(x * x, axis=1, keepdims=True) + EPS)
    unit = x * r
    gain_ref[pl.ds(0, 1), :] = jnp.sum(grad_normed * unit, axis=0, keepdims=True)
    g = grad_normed * ga_ref[...]
    gtok_ref[0] = (
        gh_ref[...] + r * (g - unit * jnp.mean(g * unit, axis=1, keepdims=True))
    ).astype(BF16)


def backward(m, slot, seg, tokens, cot, back, saved, wq, wk, wv, wo, ga, gf, held, dep):
    micro, n, d = tokens.shape
    normed, q, k, v, lse, _, hidden = saved
    mat = pl.BlockSpec((1, n, d), lambda i: (m, 0, 0))
    extra = [dep] if held is None else [dep, held]
    return pl.pallas_call(
        functools.partial(backward_kernel, m),
        grid=(1,),
        in_specs=[full(1, n), full(*seg.shape), mat, mat, full(*back.shape)]
        + [full(*a.shape) for a in (normed, q, k, v, lse, hidden)]
        + [full(d, d)] * 4 + [full(1, d)] * 2 + [ANY] * len(extra),
        out_specs=[mat] + [full(n, d)] * 4 + [full(8, d)],
        out_shape=[jax.ShapeDtypeStruct((micro, n, d), BF16)]
        + [jax.ShapeDtypeStruct((n, d), BF16)] * 4
        + [jax.ShapeDtypeStruct((8, d), F32)],
        scratch_shapes=[
            pltpu.VMEM((n, n), F32), pltpu.VMEM((n, d), BF16), pltpu.VMEM((n, d), F32)
        ],
        compiler_params=params(1),
        input_output_aliases={} if held is None else {18: 0},
    )(slot, seg, tokens, cot, back, normed, q, k, v, lse, hidden, wq, wk, wv, wo, ga, gf, *extra)


def weights_kernel(n0, n1, x0, x1, q0, q1, k0, k1, v0, v1, a0, a1, gain0, gain1, dep_ref, o_ref):
    d = n0.shape[1]
    for i, (l0, l1, r0, r1) in enumerate(
        ((n0, n1, q0, q1), (n0, n1, k0, k1), (n0, n1, v0, v1), (x0, x1, a0, a1))
    ):
        both = dot(l0[...], r0[...], 0, 0) + dot(l1[...], r1[...], 0, 0)
        o_ref[pl.ds(i * d, d), :] = both.astype(BF16)
    rest = o_ref.shape[0] - 4 * d
    line = iota((rest, d), 0)
    gain = gain0[...] + gain1[...]
    o_ref[pl.ds(4 * d, rest), :] = jnp.where(
        line == 0, gain[0:1, :], jnp.where(line == 1, gain[1:2, :], 0.0)
    ).astype(BF16)


def dense_grads(saved, grads, rest, dep):
    n, d = saved[0][0].shape
    pairs = [(saved[0][0], saved[1][0]), (saved[0][5], saved[1][5])]
    pairs += [(grads[0][i], grads[1][i]) for i in (1, 2, 3, 0, 4)]
    flat = [a for both in pairs for a in both]
    return pl.pallas_call(
        weights_kernel,
        grid=(1,),
        in_specs=[full(*a.shape) for a in flat] + [ANY],
        out_specs=full(4 * d + rest, d),
        out_shape=jax.ShapeDtypeStruct((4 * d + rest, d), BF16),
        compiler_params=params(1),
    )(*flat, dep)


def output_kernel(s0_ref, s1_ref, b0_ref, b1_ref, h0_ref, h1_ref, dep_ref, o_ref):
    n = o_ref.shape[1]
    for m, (s_ref, b_ref, h_ref) in enumerate(((s0_ref, b0_ref, h0_ref), (s1_ref, b1_ref, h1_ref))):
        places = (iota((n, b_ref.shape[0]), 1) == to_column(s_ref[...])).astype(BF16)
        o_ref[m] = (h_ref[...] + dot(places, b_ref[...])).astype(BF16)


def block_output(slots, backs, hiddens, dep):
    micro = len(slots)
    n, d = hiddens[0].shape
    flat = [*slots, *backs, *hiddens]
    return pl.pallas_call(
        output_kernel,
        grid=(1,),
        in_specs=[full(*a.shape) for a in flat] + [ANY],
        out_specs=full(micro, n, d),
        out_shape=jax.ShapeDtypeStruct((micro, n, d), BF16),
        compiler_params=params(1),
    )(*flat, dep)


def add_kernel(a_ref, b_ref, dep_ref, o_ref):
    o_ref[...] = (a_ref[...].astype(F32) + b_ref[...].astype(F32)).astype(BF16)


def add(a, b, dep):
    rows, d = a.shape
    blk = 2 * BLOCK if rows % (2 * BLOCK) == 0 else rows
    spec = pl.BlockSpec((blk, d), lambda i: (i, 0))
    return pl.pallas_call(
        add_kernel,
        grid=(rows // blk,),
        in_specs=[spec, spec, ANY],
        out_specs=spec,
        out_shape=jax.ShapeDtypeStruct((rows, d), BF16),
        compiler_params=params(1),
    )(a, b, dep)


def pick_kernel(flag_ref, a_ref, b_ref, dep_ref, o_ref):
    o_ref[...] = jnp.where(flag_ref[0] == 1, b_ref[...], a_ref[...])


def pick(flag, a, b, dep):
    return pl.pallas_call(
        pick_kernel,
        in_specs=[pl.BlockSpec(memory_space=pltpu.SMEM)]
        + [pl.BlockSpec(memory_space=pltpu.VMEM)] * 2 + [ANY],
        out_specs=pl.BlockSpec(memory_space=pltpu.VMEM),
        out_shape=jax.ShapeDtypeStruct(a.shape, BF16),
        compiler_params=params(0),
    )(flag, a, b, dep)


def store_kernel(flag_ref, a_ref, b_ref, *rest):
    gin_ref, gout_ref = rest[-2:]
    f = gout_ref.shape[1]

    def put(ref):
        gout_ref[0] = ref[pl.ds(0, f), :].astype(F32)
        gin_ref[0] = ref[pl.ds(f, f), :].astype(F32).T

    @pl.when(flag_ref[0] == 1)
    def _():
        put(b_ref)

    @pl.when(flag_ref[0] != 1)
    def _():
        put(a_ref)


def store(c, flag, a, b, ff, held, dep):
    rows, d = a.shape
    f = BLOCK
    spec = pl.BlockSpec((2 * f, d), lambda i: (i, 0))
    extra = ([] if held is None else list(held)) + [dep]
    return pl.pallas_call(
        store_kernel,
        grid=(rows // (2 * f),),
        in_specs=[pl.BlockSpec(memory_space=pltpu.SMEM), spec, spec] + [ANY] * len(extra),
        out_specs=[
            pl.BlockSpec((1, d, f), lambda i: (0, 0, c + i)),
            pl.BlockSpec((1, f, d), lambda i: (0, c + i, 0)),
        ],
        out_shape=[
            jax.ShapeDtypeStruct((1, d, ff), F32),
            jax.ShapeDtypeStruct((1, ff, d), F32),
        ],
        input_output_aliases={} if held is None else {3: 0, 4: 1},
        compiler_params=params(1),
    )(flag, a, b, *extra)


SIZES = (1, 1, 2, 2, 2, 2, 1, 1)


PLAN = (
    ("E", 0), ("S1", 0), ("E", 1), ("S1", 1), ("E", 2), ("E", 3), ("S1", 2), ("G1", 0), ("E", 4),
    ("S1", 3), ("G1", 1), ("E", 5), ("G2", 0), ("E", 6), ("E", 7), ("G2", 1), ("Q1", 0), ("G3", 0),
    ("Q1", 1), ("G3", 1), ("S1", 4), ("G1", 2), ("B", 0), ("S1", 5), ("G1", 3), ("B", 1), ("W", 0),
    ("G2", 2), ("Q2", 0), ("S1", 6), ("G1", 4), ("Q2", 1), ("G2", 3), ("S1", 7), ("G1", 5), ("O",
    0), ("G3", 2), ("G1", 6), ("S1", "A"), ("G1", 7), ("G1", "A"), ("G3", 3), ("G2", 4), ("G2", 6),
    ("G3", 4), ("G2", "A"), ("G2", 7), ("G2", 5), ("G3", 6), ("G3", "A"), ("G3", 7), ("G3", 5),
)


def per_device(
    tokens, cotangent, token_ids, hash_table, segment_ids, query_weight, key_weight,
    value_weight, output_weight, gain_attn, gain_ffn, expert_in, expert_out,
):
    micro, n, d = tokens.shape
    ff = expert_in.shape[2]
    owners = lax.axis_size("expert")
    depth = lax.axis_size("dp")
    cap = 2 * n // owners
    weights = (query_weight, key_weight, value_weight, output_weight)
    gains = (gain_attn.reshape(1, d), gain_ffn.reshape(1, d))
    place = lax.axis_index("dp")
    outer = ((place == 0) | (place == depth - 1)).astype(jnp.int32).reshape(1)
    size = hash_table.shape[0]
    table_rows = -(-size // 1024) * 8
    table = jnp.pad(hash_table, (0, table_rows * 128 - size)).reshape(table_rows, 128)

    def swap(x):
        return lax.all_to_all(x, "expert", split_axis=0, concat_axis=0, tiled=True)

    def after(x, dep):
        return lax.optimization_barrier((x, dep))[0]

    slots, saved, rx, gx = [], [], [], []
    dep = None
    for m in range(micro):
        slot, packed = route(m, token_ids, table, cotangent, owners, cap)
        gx.append(swap(packed))
        dep = packed if dep is None else dep
        *kept, packed = forward(
            m, slot, segment_ids, tokens, *weights, *gains, owners * cap, dep
        )
        rx.append(swap(packed))
        dep = packed
        slots.append(slot)
        saved.append(tuple(kept))

    starts = [sum(SIZES[:i]) for i in range(len(SIZES))]
    chunk, hop1, hop2, hop3, sum1, total = {}, {}, {}, {}, {}, {}
    held = stored = gtok = None
    backs, results, grads = {}, {}, {}
    dense = block_out = None
    for op, c in PLAN:
        if op == "E":
            chunk[c], *held = expert(
                starts[c], SIZES[c], rx, gx, expert_in, expert_out, held, dep
            )
            dep = chunk[c]
        elif op == "S1":
            x = after(chunk[c], dep)
            if depth == 4:
                hop1[c] = lax.ppermute(x, "dp", [(0, 1), (3, 2)])
            else:
                hop1[c] = x
        elif op == "G1":
            if depth == 4:
                sum1[c] = add(chunk[c], hop1[c], dep)
                hop2[c] = lax.ppermute(sum1[c], "dp", [(1, 2), (2, 1)])
                dep = sum1[c]
        elif op == "G2":
            if depth == 4:
                total[c] = add(sum1[c], hop2[c], dep)
                hop3[c] = lax.ppermute(total[c], "dp", [(1, 0), (2, 3)])
                dep = total[c]
            else:
                total[c] = hop3[c] = lax.psum(hop1[c], "dp")
        elif op == "G3":
            if c == "A":
                dense = pick(outer, total[c], hop3[c], dep)
                dep = dense
                dense = lax.all_gather(dense, "expert", axis=0, tiled=True)
            else:
                stored = store(starts[c], outer, total[c], hop3[c], ff, stored, dep)
                dep = stored[0]
        elif op == "Q1":
            dep = back_rows(c, held[1], expert_in, 1, dep)
            backs[c] = swap(dep)
        elif op == "Q2":
            dep = back_rows(c, held[0], expert_out, 0, dep)
            results[c] = swap(dep)
        elif op == "B":
            gtok, *grads[c] = backward(
                c, slots[c], segment_ids, tokens, cotangent, backs[c], saved[c], *weights,
                *gains, gtok, dep,
            )
            dep = grads[c][0]
        elif op == "W":
            dep = dense_grads(saved, grads, 16 * owners, dep)
            chunk["A"] = lax.psum_scatter(dep, "expert", scatter_dimension=0, tiled=True)
        elif op == "O":
            block_out = block_output(
                slots, [results[m] for m in range(micro)], [s[6] for s in saved], dep
            )
            dep = block_out
    wide = dense.astype(F32)
    return (
        block_out,
        gtok,
        *(wide[i * d : (i + 1) * d] for i in range(4)),
        wide[4 * d],
        wide[4 * d + 1],
        *stored,
    )


def solution(mesh):
    blocks, ids = P(None, ("dp", "expert"), None), P(None, ("dp", "expert"))
    owned = P("expert", None, None)
    return jax.shard_map(
        per_device,
        mesh=mesh,
        in_specs=(blocks, blocks, ids, P(), ids, P(), P(), P(), P(), P(), P(), owned, owned),
        out_specs=(blocks, blocks, P(), P(), P(), P(), P(), P(), owned, owned),
        check_vma=False,
    )
```

time: 799 us -> 690 us (0.86)
  Pallas kernels: 0 us -> 251 us
  waiting for transfers between devices: 397 us -> 194 us
  matrix products: 184 us -> 0 us
  starting transfers between devices: 35.6 us -> 101 us
  other arithmetic: 49.6 us -> 3.31 us
  blocking collectives: 46.7 us -> 82.1 us
  local copies, waits for them, and re-layouts: 61.3 us -> 33.3 us
    psum x2 -> x0, waiting for transfers between devices: 382 us -> none  [the longest x1 197 us: per_device(): lax.psum(grad_in_sum.astype(jnp.bfloat16), 'dp').astype(jnp.float32)]
    pallas_call x0 -> x47, Pallas kernels: none -> 251 us  [the longest x8 61.2 us: expert(): pl.pallas_call(expert_kernel, grid=(units,), in_specs=[full(rows, d)] * 4...]
    ppermute x0 -> x27, waiting for transfers between devices: none -> 194 us  [the longest x9 152 us: per_device(): hop3[c] = lax.ppermute(total[c], 'dp', [(1, 0), (2, 3)])]
    dot_general x48 -> x0, matrix products: 184 us -> none  [the longest x2 25.3 us: per_device(): jnp.dot(active.T, grad_recv, preferred_element_type=float_type)]
    ppermute x0 -> x27, starting transfers between devices: none -> 84.9 us  [the longest x9 63.4 us: per_device(): hop1[c] = lax.ppermute(x, 'dp', [(0, 1), (3, 2)])]
    all_to_all x0 -> x4, blocking collectives: none -> 82.1 us  [swap(): return lax.all_to_all(x, 'expert', split_axis=0, concat_axis=0, tiled=True)]
    psum x1 -> x0, blocking collectives: 46.7 us -> none  [per_device(): lax.psum((dense_total[0], dense_total[1], dense_total[2], dense_total[3],...]
    gather x6 -> x0, local copies, waits for them, and re-layouts: 19.2 us -> none  [the longest x2 8.88 us: per_device(): jnp.take(returned, slot_index, axis=0).astype(float_type)]
  transfers between devices with their start and end apart: 10 -> 33, of which waited for: 4 -> 10; matrix products, arithmetic and copies ran while one was open for 31% -> 1% of each run, Pallas kernels for 0% -> 25%
where the time goes in v1:
time: 690 us; the launch traced here: 680 us
  Pallas kernels  251 us (36%)
  waiting for transfers between devices  194 us (28%)
  starting transfers between devices  101 us (15%)
  blocking collectives  82.1 us (12%)
  local copies, waits for them, and re-layouts  33.3 us (5%)
  between operations  15 us (2%)
    ppermute x9, waiting for transfers between devices, per_device(): hop3[c] = lax.ppermute(total[c], 'dp', [(1, 0), (2, 3)])  152 us
    all_to_all x4, blocking collectives, swap(): return lax.all_to_all(x, 'expert', split_axis=0, concat_axis=0, tiled=True)  82.1 us
    ppermute x9, starting transfers between devices, per_device(): hop1[c] = lax.ppermute(x, 'dp', [(0, 1), (3, 2)])  63.4 us
    pallas_call x8, Pallas kernels, expert(): pl.pallas_call(expert_kernel, grid=(units,), in_specs=[full(rows, d)] * 4...  61.2 us
    pallas_call x18, Pallas kernels, add(): pl.pallas_call(add_kernel, grid=(rows // blk,), in_specs=[spec, spec, ANY...  48.2 us
    ppermute x9, waiting for transfers between devices, per_device(): hop1[c] = lax.ppermute(x, 'dp', [(0, 1), (3, 2)])  42.3 us
    pallas_call x2, Pallas kernels, backward(): pl.pallas_call(functools.partial(backward_kernel, m), grid=(1,), in_specs...  34.9 us
    pallas_call x4, Pallas kernels, back_rows(): pl.pallas_call(functools.partial(rows_kernel, side), grid=(steps,), in_sp...  32.4 us
  transfers between devices with their start and end apart: 33, of which 10 were waited for; matrix products, arithmetic and copies ran while one was open for 1% of the time, Pallas kernels for 25%

profile of v1, /device:TPU:0, one launch (start us, length us, event | category | flops | bytes accessed | tf_op | source)
XLA Modules:
  0.0 679.8 jit_solution(1708407132600362064)
XLA Ops:
  16.2 13.3 %shard_map.206 = (bf16[384,768]{1,0:T(8,128)(2,1)}, bf16[384,768]{1,0:T(8,128)(2,1)}, bf16[384,768]{1,0:T(8,128)(2,1)}, bf16[384,768]{1,0:T(8,128)(2,1)}, f32[16...) custom-call(s32[1,384]{1,0:T(1,128)} %get-tuple-element.91.slot_ref.s0_ref, ...), custom_call_target="tpu_custom_call" | custom-call | tf_op jit(solution)/shard_map/pallas_call | solution.py:138
  29.5 13.3 %shard_map.207 = (bf16[384,768]{1,0:T(8,128)(2,1)}, bf16[384,768]{1,0:T(8,128)(2,1)}, bf16[384,768]{1,0:T(8,128)(2,1)}, bf16[384,768]{1,0:T(8,128)(2,1)}, f32[16...) custom-call(s32[1,384]{1,0:T(1,128)} %get-tuple-element.92.slot_ref.s1_ref, ...), custom_call_target="tpu_custom_call" | custom-call | tf_op jit(solution)/shard_map/pallas_call | solution.py:138
  42.9 22.2 %all_to_all.88 = bf16[8,96,768]{2,1,0:T(8,128)(2,1)} all-to-all(bf16[8,96,768]{2,1,0:T(8,128)(2,1)} %bitcast.58), channel_id=1, replica_groups=mesh['dp'=4,'expert'=8] {'expert'}, dimensions={0} | all-to-all | bytes 2359296 | tf_op jit(solution)/shard_map/all_to_all | solution.py:461
  65.1 20.0 %all_to_all.89 = bf16[8,96,768]{2,1,0:T(8,128)(2,1)} all-to-all(bf16[8,96,768]{2,1,0:T(8,128)(2,1)S(1)} %bitcast.56), channel_id=1, replica_groups=mesh['dp'=4,'expert'=8] {'expert'}, dimensions={0} | all-to-all | bytes 2359296 | tf_op jit(solution)/shard_map/all_to_all | solution.py:461
  85.1 20.0 %all_to_all.90 = bf16[8,96,768]{2,1,0:T(8,128)(2,1)} all-to-all(bf16[8,96,768]{2,1,0:T(8,128)(2,1)S(1)} %bitcast.55), channel_id=1, replica_groups=mesh['dp'=4,'expert'=8] {'expert'}, dimensions={0} | all-to-all | bytes 2359296 | tf_op jit(solution)/shard_map/all_to_all | solution.py:461
  105.1 19.9 %all_to_all.91 = bf16[8,96,768]{2,1,0:T(8,128)(2,1)} all-to-all(bf16[8,96,768]{2,1,0:T(8,128)(2,1)S(1)} %bitcast.59), channel_id=1, replica_groups=mesh['dp'=4,'expert'=8] {'expert'}, dimensions={0} | all-to-all | bytes 2359296 | tf_op jit(solution)/shard_map/all_to_all | solution.py:461
  125.0 6.2 shard_map.208
  135.3 6.2 shard_map.209
  142.8 9.1 %shard_map.210 = (bf16[1024,768]{1,0:T(8,128)(2,1)}, bf16[1536,3072]{1,0:T(8,128)(2,1)}, bf16[1536,3072]{1,0:T(8,128)(2,1)}) custom-call(bf16[768,768]{1,0:T(8,128)(2,1)} %bitcast.29, bf16[768,768]{1,0:T(8,128)(2,1)} %bitcast.21, bf16[768,768]{1,0:T(8,128)(2,1)} %bitcast.37, ...), custom_call_target="tpu_custom_call", output_to_operand_aliasing={{1}: (6, {}), {2}: (7, {})} | custom-call | tf_op jit(solution)/shard_map/pallas_call | solution.py:182
  151.9 9.1 %shard_map.211 = (bf16[1024,768]{1,0:T(8,128)(2,1)}, bf16[1536,3072]{1,0:T(8,128)(2,1)}, bf16[1536,3072]{1,0:T(8,128)(2,1)}) custom-call(bf16[768,768]{1,0:T(8,128)(2,1)} %bitcast.30, bf16[768,768]{1,0:T(8,128)(2,1)} %bitcast.22, bf16[768,768]{1,0:T(8,128)(2,1)} %bitcast.38, ...), custom_call_target="tpu_custom_call", output_to_operand_aliasing={{1}: (6, {}), {2}: (7, {})} | custom-call | tf_op jit(solution)/shard_map/pallas_call | solution.py:182
  165.1 9.1 %shard_map.213 = (bf16[1024,768]{1,0:T(8,128)(2,1)}, bf16[1536,3072]{1,0:T(8,128)(2,1)}, bf16[1536,3072]{1,0:T(8,128)(2,1)}) custom-call(bf16[768,768]{1,0:T(8,128)(2,1)} %bitcast.31, bf16[768,768]{1,0:T(8,128)(2,1)} %bitcast.23, bf16[768,768]{1,0:T(8,128)(2,1)} %bitcast.39, ...), custom_call_target="tpu_custom_call", output_to_operand_aliasing={{1}: (6, {}), {2}: (7, {})} | custom-call | tf_op jit(solution)/shard_map/pallas_call | solution.py:182
  178.7 9.1 %shard_map.215 = (bf16[1024,768]{1,0:T(8,128)(2,1)}, bf16[1536,3072]{1,0:T(8,128)(2,1)}, bf16[1536,3072]{1,0:T(8,128)(2,1)}) custom-call(bf16[768,768]{1,0:T(8,128)(2,1)} %bitcast.32, bf16[768,768]{1,0:T(8,128)(2,1)} %bitcast.24, bf16[768,768]{1,0:T(8,128)(2,1)} %bitcast.40, ...), custom_call_target="tpu_custom_call", output_to_operand_aliasing={{1}: (6, {}), {2}: (7, {})} | custom-call | tf_op jit(solution)/shard_map/pallas_call | solution.py:182
  197.3 6.2 shard_map.218
  206.8 7.9 %shard_map.220.rest_0_ = bf16[768,768]{1,0:T(8,128)(2,1)} custom-call(bf16[1536,3072]{1,0:T(8,128)(2,1)} %get-tuple-element.123.a_ref, bf16[1,768,3072]{2,1,0:T(8,128)(2,1)} %w_ref.5, bf16[512,768]{1,0:T(8,128)(2,1)} %shard_map.219.dep_ref.a_ref), custom_call_target="tpu_custom_call" | custom-call | tf_op jit(solution)/shard_map/pallas_call | solution.py:215
  219.8 7.7 %collective-permute-start.3 = (bf16[1024,768]{1,0:T(8,128)(2,1)S(1)}, bf16[1024,768]{1,0:T(8,128)(2,1)}, u32[]{:S(2)}, u32[]{:S(2)}) collective-permute-start(bf16[1024,768]{1,0:T(8,128)(2,1)S(1)} %copy-done.11), channel_id=1, source_target_pairs={{0,8},{24,16},{1,9},{25,17},{2,10},{26,18},{3,11},{27,19},{4,12},{... | collective-permute-start | bytes 4718600 | tf_op jit(solution)/shard_map/ppermute | solution.py:494
  229.9 11.8 %collective-permute-done.6.b_ref = bf16[512,768]{1,0:T(8,128)(2,1)} collective-permute-done((bf16[512,768]{1,0:T(8,128)(2,1)S(1)}, bf16[512,768]{1,0:T(8,128)(2,1)}, u32[]{:S(2)}, u32[]{:S(2)}) %collective-permute-start.6) | collective-permute-done | bytes 786464 | tf_op jit(solution)/shard_map/ppermute | solution.py:505
  244.4 8.0 %shard_map.222.rest_2_ = bf16[768,768]{1,0:T(8,128)(2,1)} custom-call(bf16[1536,3072]{1,0:T(8,128)(2,1)} %get-tuple-element.123.a_ref, bf16[1,768,3072]{2,1,0:T(8,128)(2,1)} %w_ref.5, f32[1,768,3072]{2,1,0:T(8,128)} %get-tuple-element.124.dep_ref.rest_0_), custom_call_target="tpu_custom_call" | custom-call | tf_op jit(solution)/shard_map/pallas_call | solution.py:215
  258.1 20.4 %collective-permute-done.5.b_ref = bf16[512,768]{1,0:T(8,128)(2,1)S(1)} collective-permute-done((bf16[512,768]{1,0:T(8,128)(2,1)S(1)}, bf16[512,768]{1,0:T(8,128)(2,1)S(1)}, u32[]{:S(2)}, u32[]{:S(2)}) %collective-permute-start.5) | collective-permute-done | bytes 786464 | tf_op jit(solution)/shard_map/ppermute | solution.py:505
  285.2 17.4 %shard_map.225 = (bf16[2,384,768]{2,1,0:T(8,128)(2,1)}, bf16[384,768]{1,0:T(8,128)(2,1)}, bf16[384,768]{1,0:T(8,128)(2,1)}, bf16[384,768]{1,0:T(8,128)(2,1)}, bf...) custom-call(s32[1,384]{1,0:T(1,128)} %get-tuple-element.91.slot_ref.s0_ref, s32[2,384]{1,0:T(2,128)} %seg_ref.7, ...), custom_call_target="tpu_custom_call" | custom-call | tf_op jit(solution)/shard_map/pallas_call | solution.py:289
  305.5 17.6 %shard_map.227 = (bf16[2,384,768]{2,1,0:T(8,128)(2,1)}, bf16[384,768]{1,0:T(8,128)(2,1)}, bf16[384,768]{1,0:T(8,128)(2,1)}, bf16[384,768]{1,0:T(8,128)(2,1)}, bf...) custom-call(s32[1,384]{1,0:T(1,128)} %get-tuple-element.92.slot_ref.s1_ref, ...), custom_call_target="tpu_custom_call", output_to_operand_aliasing={{0}: (18, {})} | custom-call | tf_op jit(solution)/shard_map/pallas_call | solution.py:289
  323.1 10.3 %shard_map.228.dep_ref = bf16[3200,768]{1,0:T(8,128)(2,1)} custom-call(bf16[384,768]{1,0:T(8,128)(2,1)} %get-tuple-element.127.normed_ref.n0, bf16[384,768]{1,0:T(8,128)(2,1)} %get-tuple-element.128.normed_ref.n1, bf16[384,768]{1,0:T(8,128)(2,1)} %get-tuple-element.129.x0, bf16[384,768]{1,0:T(8,128)(2,1)} %get-tuple-element.130.x1, ...), custom_call_target="tpu_custom_call" | custom-call | tf_op jit(solution)/shard_map/pallas_call | solution.py:327
  346.1 8.2 %shard_map.230.dep_ref = bf16[768,768]{1,0:T(8,128)(2,1)} custom-call(bf16[1536,3072]{1,0:T(8,128)(2,1)} %get-tuple-element.120.a_ref, bf16[1,3072,768]{2,1,0:T(8,128)(2,1)} %w_ref.7, bf16[1024,768]{1,0:T(8,128)(2,1)} %shard_map.229.dep_ref.a_ref), custom_call_target="tpu_custom_call" | custom-call | tf_op jit(solution)/shard_map/pallas_call | solution.py:215
  354.3 18.5 %collective-permute-done.9.b_ref = bf16[1024,768]{1,0:T(8,128)(2,1)S(1)} collective-permute-done((bf16[1024,768]{1,0:T(8,128)(2,1)S(1)}, bf16[1024,768]{1,0:T(8,128)(2,1)S(1)}, u32[]{:S(2)}, u32[]{:S(2)}) %collective-permute-start.9) | collective-permute-done | bytes 1572896 | tf_op jit(solution)/shard_map/ppermute | solution.py:494
  376.9 8.3 %shard_map.232.dep_ref = bf16[768,768]{1,0:T(8,128)(2,1)} custom-call(bf16[1536,3072]{1,0:T(8,128)(2,1)} %get-tuple-element.120.a_ref, bf16[1,3072,768]{2,1,0:T(8,128)(2,1)} %w_ref.7, bf16[1024,768]{1,0:T(8,128)(2,1)} %shard_map.231.dep_ref.a_ref), custom_call_target="tpu_custom_call" | custom-call | tf_op jit(solution)/shard_map/pallas_call | solution.py:215
  388.9 15.7 %collective-permute-start.10 = (bf16[1024,768]{1,0:T(8,128)(2,1)}, bf16[1024,768]{1,0:T(8,128)(2,1)}, u32[]{:S(2)}, u32[]{:S(2)}) collective-permute-start(bf16[1024,768]{1,0:T(8,128)(2,1)} %get-tuple-element.154.dep_ref.a_ref), channel_id=1, source_target_pairs={{0,8},{24,16},{1,9},{25,17},{2,10},{26,18},{3,11},{27,19},{4,12},{... | collective-permute-start | bytes 4718600 | tf_op jit(solution)/shard_map/ppermute | solution.py:494
  417.4 18.2 %collective-permute-start.12 = (bf16[512,768]{1,0:T(8,128)(2,1)}, bf16[512,768]{1,0:T(8,128)(2,1)}, u32[]{:S(2)}, u32[]{:S(2)}) collective-permute-start(bf16[512,768]{1,0:T(8,128)(2,1)} %get-tuple-element.156.rest_2_.a_ref), channel_id=1, source_target_pairs={{0,8},{24,16},{1,9},{25,17},{2,10},{26,18},{3,11},{27,19},{4,12},{... | collective-permute-start | bytes 2359304 | tf_op jit(solution)/shard_map/ppermute | solution.py:494
  462.1 10.0 %collective-permute-done.15.b_ref = bf16[512,768]{1,0:T(8,128)(2,1)} collective-permute-done((bf16[512,768]{1,0:T(8,128)(2,1)}, bf16[512,768]{1,0:T(8,128)(2,1)}, u32[]{:S(2)}, u32[]{:S(2)}) %collective-permute-start.15) | collective-permute-done | bytes 786464 | tf_op jit(solution)/shard_map/ppermute | solution.py:494
  474.6 10.4 %collective-permute-done.14.b_ref = bf16[400,768]{1,0:T(8,128)(2,1)S(1)} collective-permute-done((bf16[400,768]{1,0:T(8,128)(2,1)}, bf16[400,768]{1,0:T(8,128)(2,1)S(1)}, u32[]{:S(2)}, u32[]{:S(2)}) %collective-permute-start.14) | collective-permute-done | bytes 614432 | tf_op jit(solution)/shard_map/ppermute | solution.py:494
  503.1 30.6 %collective-permute-done.19.b_ref = bf16[1024,768]{1,0:T(8,128)(2,1)S(1)} collective-permute-done((bf16[1024,768]{1,0:T(8,128)(2,1)}, bf16[1024,768]{1,0:T(8,128)(2,1)S(1)}, u32[]{:S(2)}, u32[]{:S(2)}) %collective-permute-start.19) | collective-permute-done | bytes 1572896 | tf_op jit(solution)/shard_map/ppermute | solution.py:505
  553.4 29.7 %collective-permute-done.21.b_ref = bf16[400,768]{1,0:T(8,128)(2,1)S(1)} collective-permute-done((bf16[400,768]{1,0:T(8,128)(2,1)}, bf16[400,768]{1,0:T(8,128)(2,1)S(1)}, u32[]{:S(2)}, u32[]{:S(2)}) %collective-permute-start.21) | collective-permute-done | bytes 614432 | tf_op jit(solution)/shard_map/ppermute | solution.py:505
  588.9 59.3 %collective-permute-done.26.b_ref = bf16[512,768]{1,0:T(8,128)(2,1)S(1)} collective-permute-done((bf16[512,768]{1,0:T(8,128)(2,1)S(1)}, bf16[512,768]{1,0:T(8,128)(2,1)S(1)}, u32[]{:S(2)}, u32[]{:S(2)}) %collective-permute-start.26) | collective-permute-done | bytes 786464 | tf_op jit(solution)/shard_map/ppermute | solution.py:505
  651.8 8.6 %copy.79.rest_0_ = f32[1,768,3072]{2,1,0:T(8,128)} copy(f32[1,768,3072]{2,1,0:T(8,128)} %get-tuple-element.168.rest_2_) | data formatting | bytes 18874368
  (168 shorter events, 182.6 us)
Async XLA Ops:
  131.2 29.9 %collective-permute-start = (bf16[512,768]{1,0:T(8,128)(2,1)}, bf16[512,768]{1,0:T(8,128)(2,1)S(1)}, u32[]{:S(2)}, u32[]{:S(2)}) collective-permute-start(bf16[512,768]{1,0:T(8,128)(2,1)} %get-tuple-element.108.rest_2_.a_ref), channel_id=1, source_target_pairs={{0,8},{24,16},{1,9},{25,17},{2,10},{26,18},{3,11},{27,19},{4,12},{... | collective-permute-start | bytes 2359304 | tf_op jit(solution)/shard_map/ppermute | solution.py:494
  141.5 32.7 %collective-permute-start.1 = (bf16[512,768]{1,0:T(8,128)(2,1)}, bf16[512,768]{1,0:T(8,128)(2,1)S(1)}, u32[]{:S(2)}, u32[]{:S(2)}) collective-permute-start(bf16[512,768]{1,0:T(8,128)(2,1)} %get-tuple-element.112.rest_2_.a_ref), channel_id=1, source_target_pairs={{0,8},{24,16},{1,9},{25,17},{2,10},{26,18},{3,11},{27,19},{4,12},{... | collective-permute-start | bytes 2359304 | tf_op jit(solution)/shard_map/ppermute | solution.py:494
  164.3 23.5 %collective-permute-start.2 = (bf16[512,768]{1,0:T(8,128)(2,1)}, bf16[512,768]{1,0:T(8,128)(2,1)S(1)}, u32[]{:S(2)}, u32[]{:S(2)}) collective-permute-start(bf16[512,768]{1,0:T(8,128)(2,1)} %shard_map.212.rest_2_.a_ref), channel_id=1, source_target_pairs={{8,16},{16,8},{9,17},{17,9},{10,18},{18,10},{11,19},{19,11},{12,20... | collective-permute-start | bytes 2359304 | tf_op jit(solution)/shard_map/ppermute | solution.py:500
  177.6 25.9 %collective-permute-start.4 = (bf16[512,768]{1,0:T(8,128)(2,1)}, bf16[512,768]{1,0:T(8,128)(2,1)S(1)}, u32[]{:S(2)}, u32[]{:S(2)}) collective-permute-start(bf16[512,768]{1,0:T(8,128)(2,1)} %shard_map.214.rest_2_.a_ref), channel_id=1, source_target_pairs={{8,16},{16,8},{9,17},{17,9},{10,18},{18,10},{11,19},{19,11},{12,20... | collective-permute-start | bytes 2359304 | tf_op jit(solution)/shard_map/ppermute | solution.py:500
  214.8 37.6 %all-to-all-start.4 = ((bf16[8,96,768]{2,1,0:T(8,128)(2,1)}), bf16[8,96,768]{2,1,0:T(8,128)(2,1)S(1)}, u32[]{:S(2)}, u32[]{:S(2)}) async-start(bf16[8,96,768]{2,1,0:T(8,128)(2,1)} %bitcast.53), calls=%async_computation.4 | async-start | bytes 2359296 | tf_op jit(solution)/shard_map/all_to_all | solution.py:461
  218.5 23.2 %collective-permute-start.6 = (bf16[512,768]{1,0:T(8,128)(2,1)S(1)}, bf16[512,768]{1,0:T(8,128)(2,1)}, u32[]{:S(2)}, u32[]{:S(2)}) collective-permute-start(bf16[512,768]{1,0:T(8,128)(2,1)S(1)} %copy-done.10), channel_id=1, source_target_pairs={{8,0},{16,24},{9,1},{17,25},{10,2},{18,26},{11,3},{19,27},{12,4},{... | collective-permute-start | bytes 2359304 | tf_op jit(solution)/shard_map/ppermute | solution.py:505
  219.8 62.4 %collective-permute-start.3 = (bf16[1024,768]{1,0:T(8,128)(2,1)S(1)}, bf16[1024,768]{1,0:T(8,128)(2,1)}, u32[]{:S(2)}, u32[]{:S(2)}) collective-permute-start(bf16[1024,768]{1,0:T(8,128)(2,1)S(1)} %copy-done.11), channel_id=1, source_target_pairs={{0,8},{24,16},{1,9},{25,17},{2,10},{26,18},{3,11},{27,19},{4,12},{... | collective-permute-start | bytes 4718600 | tf_op jit(solution)/shard_map/ppermute | solution.py:494
  227.5 75.0 %collective-permute-start.8 = (bf16[1024,768]{1,0:T(8,128)(2,1)}, bf16[1024,768]{1,0:T(8,128)(2,1)}, u32[]{:S(2)}, u32[]{:S(2)}) collective-permute-start(bf16[1024,768]{1,0:T(8,128)(2,1)} %get-tuple-element.142.dep_ref.a_ref), channel_id=1, source_target_pairs={{0,8},{24,16},{1,9},{25,17},{2,10},{26,18},{3,11},{27,19},{4,12},{... | collective-permute-start | bytes 4718600 | tf_op jit(solution)/shard_map/ppermute | solution.py:494
  252.4 53.2 %all-to-all-start.5 = ((bf16[8,96,768]{2,1,0:T(8,128)(2,1)}), bf16[8,96,768]{2,1,0:T(8,128)(2,1)}, u32[]{:S(2)}, u32[]{:S(2)}) async-start(bf16[8,96,768]{2,1,0:T(8,128)(2,1)} %bitcast.51), calls=%async_computation.5 | async-start | bytes 2359296 | tf_op jit(solution)/shard_map/all_to_all | solution.py:461
  256.8 201.0 %reduce-scatter.2.cloned.1.call-start = ((), (), s32[]{:S(2)}) async-start(), calls=%async_computation.9 | async-start | bytes 5529600 | tf_op jit(solution)/shard_map/reduce_scatter | solution.py:531
  256.8 21.7 %collective-permute-start.5 = (bf16[512,768]{1,0:T(8,128)(2,1)S(1)}, bf16[512,768]{1,0:T(8,128)(2,1)S(1)}, u32[]{:S(2)}, u32[]{:S(2)}) collective-permute-start(bf16[512,768]{1,0:T(8,128)(2,1)S(1)} %copy-done.6), channel_id=1, source_target_pairs={{8,0},{16,24},{9,1},{17,25},{10,2},{18,26},{11,3},{19,27},{12,4},{... | collective-permute-start | bytes 2359304 | tf_op jit(solution)/shard_map/ppermute | solution.py:505
  334.8 6.9 %collective-permute-start.7 = (bf16[1024,768]{1,0:T(8,128)(2,1)S(1)}, bf16[1024,768]{1,0:T(8,128)(2,1)S(1)}, u32[]{:S(2)}, u32[]{:S(2)}) collective-permute-start(bf16[1024,768]{1,0:T(8,128)(2,1)S(1)} %copy-done.4), channel_id=1, source_target_pairs={{8,16},{16,8},{9,17},{17,9},{10,18},{18,10},{11,19},{19,11},{12,20... | collective-permute-start | bytes 4718600 | tf_op jit(solution)/shard_map/ppermute | solution.py:500
  335.6 37.2 %collective-permute-start.9 = (bf16[1024,768]{1,0:T(8,128)(2,1)S(1)}, bf16[1024,768]{1,0:T(8,128)(2,1)S(1)}, u32[]{:S(2)}, u32[]{:S(2)}) collective-permute-start(bf16[1024,768]{1,0:T(8,128)(2,1)S(1)} %copy-done.12), channel_id=1, source_target_pairs={{0,8},{24,16},{1,9},{25,17},{2,10},{26,18},{3,11},{27,19},{4,12},{... | collective-permute-start | bytes 4718600 | tf_op jit(solution)/shard_map/ppermute | solution.py:494
  339.9 71.4 %collective-permute-start.11 = (bf16[1024,768]{1,0:T(8,128)(2,1)}, bf16[1024,768]{1,0:T(8,128)(2,1)}, u32[]{:S(2)}, u32[]{:S(2)}) collective-permute-start(bf16[1024,768]{1,0:T(8,128)(2,1)} %shard_map.226.rest_0_.a_ref), channel_id=1, source_target_pairs={{8,16},{16,8},{9,17},{17,9},{10,18},{18,10},{11,19},{19,11},{12,20... | collective-permute-start | bytes 4718600 | tf_op jit(solution)/shard_map/ppermute | solution.py:500
  385.1 20.8 %all-to-all-start.7 = ((bf16[8,96,768]{2,1,0:T(8,128)(2,1)}), bf16[8,96,768]{2,1,0:T(8,128)(2,1)S(1)}, u32[]{:S(2)}, u32[]{:S(2)}) async-start(bf16[8,96,768]{2,1,0:T(8,128)(2,1)} %bitcast.52), calls=%async_computation.7 | async-start | bytes 2359296 | tf_op jit(solution)/shard_map/all_to_all | solution.py:461
  388.9 49.5 %collective-permute-start.10 = (bf16[1024,768]{1,0:T(8,128)(2,1)}, bf16[1024,768]{1,0:T(8,128)(2,1)}, u32[]{:S(2)}, u32[]{:S(2)}) collective-permute-start(bf16[1024,768]{1,0:T(8,128)(2,1)} %get-tuple-element.154.dep_ref.a_ref), channel_id=1, source_target_pairs={{0,8},{24,16},{1,9},{25,17},{2,10},{26,18},{3,11},{27,19},{4,12},{... | collective-permute-start | bytes 4718600 | tf_op jit(solution)/shard_map/ppermute | solution.py:494
  404.6 46.8 %collective-permute-start.13 = (bf16[1024,768]{1,0:T(8,128)(2,1)S(1)}, bf16[1024,768]{1,0:T(8,128)(2,1)}, u32[]{:S(2)}, u32[]{:S(2)}) collective-permute-start(bf16[1024,768]{1,0:T(8,128)(2,1)S(1)} %copy-done.2), channel_id=1, source_target_pairs={{8,0},{16,24},{9,1},{17,25},{10,2},{18,26},{11,3},{19,27},{12,4},{... | collective-permute-start | bytes 4718600 | tf_op jit(solution)/shard_map/ppermute | solution.py:505
  406.9 39.9 %all-to-all-start.6 = ((bf16[8,96,768]{2,1,0:T(8,128)(2,1)}), bf16[8,96,768]{2,1,0:T(8,128)(2,1)}, u32[]{:S(2)}, u32[]{:S(2)}) async-start(bf16[8,96,768]{2,1,0:T(8,128)(2,1)} %bitcast.14), calls=%async_computation.6 | async-start | bytes 2359296 | tf_op jit(solution)/shard_map/all_to_all | solution.py:461
  411.2 253.6 %all-gather.2.cloned.1.call-start = ((), (), s32[]{:S(2)}) async-start(), calls=%async_computation.10 | async-start | bytes 5529600 | tf_op jit(solution)/shard_map/all_gather | solution.py:513
  414.3 73.7 %collective-permute-start.18 = (bf16[1024,768]{1,0:T(8,128)(2,1)}, bf16[1024,768]{1,0:T(8,128)(2,1)}, u32[]{:S(2)}, u32[]{:S(2)}) collective-permute-start(bf16[1024,768]{1,0:T(8,128)(2,1)} %shard_map.233.dep_ref.a_ref), channel_id=1, source_target_pairs={{8,0},{16,24},{9,1},{17,25},{10,2},{18,26},{11,3},{19,27},{12,4},{... | collective-permute-start | bytes 4718600 | tf_op jit(solution)/shard_map/ppermute | solution.py:505
  415.6 75.7 %collective-permute-start.17 = (bf16[1024,768]{1,0:T(8,128)(2,1)S(1)}, bf16[1024,768]{1,0:T(8,128)(2,1)}, u32[]{:S(2)}, u32[]{:S(2)}) collective-permute-start(bf16[1024,768]{1,0:T(8,128)(2,1)S(1)} %copy-done.3), channel_id=1, source_target_pairs={{8,16},{16,8},{9,17},{17,9},{10,18},{18,10},{11,19},{19,11},{12,20... | collective-permute-start | bytes 4718600 | tf_op jit(solution)/shard_map/ppermute | solution.py:500
  417.4 37.9 %collective-permute-start.12 = (bf16[512,768]{1,0:T(8,128)(2,1)}, bf16[512,768]{1,0:T(8,128)(2,1)}, u32[]{:S(2)}, u32[]{:S(2)}) collective-permute-start(bf16[512,768]{1,0:T(8,128)(2,1)} %get-tuple-element.156.rest_2_.a_ref), channel_id=1, source_target_pairs={{0,8},{24,16},{1,9},{25,17},{2,10},{26,18},{3,11},{27,19},{4,12},{... | collective-permute-start | bytes 2359304 | tf_op jit(solution)/shard_map/ppermute | solution.py:494
  438.4 33.7 %collective-permute-start.15 = (bf16[512,768]{1,0:T(8,128)(2,1)}, bf16[512,768]{1,0:T(8,128)(2,1)}, u32[]{:S(2)}, u32[]{:S(2)}) collective-permute-start(bf16[512,768]{1,0:T(8,128)(2,1)} %get-tuple-element.160.dep_ref.a_ref), channel_id=1, source_target_pairs={{0,8},{24,16},{1,9},{25,17},{2,10},{26,18},{3,11},{27,19},{4,12},{... | collective-permute-start | bytes 2359304 | tf_op jit(solution)/shard_map/ppermute | solution.py:494
  457.7 27.2 %collective-permute-start.14 = (bf16[400,768]{1,0:T(8,128)(2,1)}, bf16[400,768]{1,0:T(8,128)(2,1)S(1)}, u32[]{:S(2)}, u32[]{:S(2)}) collective-permute-start(bf16[400,768]{1,0:T(8,128)(2,1)} %reduce-scatter.2.cloned.1.call-done.a_ref), channel_id=1, source_target_pairs={{0,8},{24,16},{1,9},{25,17},{2,10},{26,18},{3,11},{27,19},{4,12},{... | collective-permute-start | bytes 1843208 | tf_op jit(solution)/shard_map/ppermute | solution.py:494
  494.3 39.4 %collective-permute-start.19 = (bf16[1024,768]{1,0:T(8,128)(2,1)}, bf16[1024,768]{1,0:T(8,128)(2,1)S(1)}, u32[]{:S(2)}, u32[]{:S(2)}) collective-permute-start(bf16[1024,768]{1,0:T(8,128)(2,1)} %shard_map.241.dep_ref.a_ref), channel_id=1, source_target_pairs={{8,0},{16,24},{9,1},{17,25},{10,2},{18,26},{11,3},{19,27},{12,4},{... | collective-permute-start | bytes 4718600 | tf_op jit(solution)/shard_map/ppermute | solution.py:505
  497.2 48.6 %collective-permute-start.23 = (bf16[1024,768]{1,0:T(8,128)(2,1)S(1)}, bf16[1024,768]{1,0:T(8,128)(2,1)S(1)}, u32[]{:S(2)}, u32[]{:S(2)}) collective-permute-start(bf16[1024,768]{1,0:T(8,128)(2,1)S(1)} %copy-done.5), channel_id=1, source_target_pairs={{8,16},{16,8},{9,17},{17,9},{10,18},{18,10},{11,19},{19,11},{12,20... | collective-permute-start | bytes 4718600 | tf_op jit(solution)/shard_map/ppermute | solution.py:500
  497.9 40.1 %collective-permute-start.16 = (bf16[400,768]{1,0:T(8,128)(2,1)S(1)}, bf16[400,768]{1,0:T(8,128)(2,1)S(1)}, u32[]{:S(2)}, u32[]{:S(2)}) collective-permute-start(bf16[400,768]{1,0:T(8,128)(2,1)S(1)} %copy-done.13), channel_id=1, source_target_pairs={{8,16},{16,8},{9,17},{17,9},{10,18},{18,10},{11,19},{19,11},{12,20... | collective-permute-start | bytes 1843208 | tf_op jit(solution)/shard_map/ppermute | solution.py:500
  498.7 43.8 %collective-permute-start.24 = (bf16[512,768]{1,0:T(8,128)(2,1)S(1)}, bf16[512,768]{1,0:T(8,128)(2,1)S(1)}, u32[]{:S(2)}, u32[]{:S(2)}) collective-permute-start(bf16[512,768]{1,0:T(8,128)(2,1)S(1)} %copy-done.8), channel_id=1, source_target_pairs={{8,16},{16,8},{9,17},{17,9},{10,18},{18,10},{11,19},{19,11},{12,20... | collective-permute-start | bytes 2359304 | tf_op jit(solution)/shard_map/ppermute | solution.py:500
  501.8 48.0 %collective-permute-start.22 = (bf16[512,768]{1,0:T(8,128)(2,1)}, bf16[512,768]{1,0:T(8,128)(2,1)S(1)}, u32[]{:S(2)}, u32[]{:S(2)}) collective-permute-start(bf16[512,768]{1,0:T(8,128)(2,1)} %shard_map.242.rest_2_.a_ref), channel_id=1, source_target_pairs={{8,0},{16,24},{9,1},{17,25},{10,2},{18,26},{11,3},{19,27},{12,4},{... | collective-permute-start | bytes 2359304 | tf_op jit(solution)/shard_map/ppermute | solution.py:505
  541.1 42.0 %collective-permute-start.21 = (bf16[400,768]{1,0:T(8,128)(2,1)}, bf16[400,768]{1,0:T(8,128)(2,1)S(1)}, u32[]{:S(2)}, u32[]{:S(2)}) collective-permute-start(bf16[400,768]{1,0:T(8,128)(2,1)} %shard_map.244.dep_ref.a_ref), channel_id=1, source_target_pairs={{8,0},{16,24},{9,1},{17,25},{10,2},{18,26},{11,3},{19,27},{12,4},{... | collective-permute-start | bytes 1843208 | tf_op jit(solution)/shard_map/ppermute | solution.py:505
  586.3 74.1 %collective-permute-start.25 = (bf16[1024,768]{1,0:T(8,128)(2,1)S(1)}, bf16[1024,768]{1,0:T(8,128)(2,1)S(1)}, u32[]{:S(2)}, u32[]{:S(2)}) collective-permute-start(bf16[1024,768]{1,0:T(8,128)(2,1)S(1)} %copy-done.1), channel_id=1, source_target_pairs={{8,0},{16,24},{9,1},{17,25},{10,2},{18,26},{11,3},{19,27},{12,4},{... | collective-permute-start | bytes 4718600 | tf_op jit(solution)/shard_map/ppermute | solution.py:505
  587.6 60.6 %collective-permute-start.26 = (bf16[512,768]{1,0:T(8,128)(2,1)S(1)}, bf16[512,768]{1,0:T(8,128)(2,1)S(1)}, u32[]{:S(2)}, u32[]{:S(2)}) collective-permute-start(bf16[512,768]{1,0:T(8,128)(2,1)S(1)} %copy-done.7), channel_id=1, source_target_pairs={{8,0},{16,24},{9,1},{17,25},{10,2},{18,26},{11,3},{19,27},{12,4},{... | collective-permute-start | bytes 2359304 | tf_op jit(solution)/shard_map/ppermute | solution.py:505
  (38 other events, 203.3 us)
Sparse Core Ops, SparseCore 0:
  333.5 55.1 reduce-scatter.1
  586.4 48.9 all-gather.1

commit v2 on v1

--- a/solution.py
+++ b/solution.py
@@ -14,17 +14,23 @@
 PAIR = 2 * HEAD_DIM
 F32 = jnp.float32
 BF16 = jnp.bfloat16
-VMEM_LIMIT = 56 * 1024 * 1024
 
 
 def dot(a, b, ca=1, cb=0):
     return lax.dot_general(a, b, (((ca,), (cb,)), ((), ())), preferred_element_type=F32)
 
 
-def params(n):
+def params(mib):
     return pltpu.CompilerParams(
-        dimension_semantics=("arbitrary",) * n, vmem_limit_bytes=VMEM_LIMIT
-    )
+        dimension_semantics=("arbitrary",), vmem_limit_bytes=mib * 1024 * 1024
+    )
+
+
+PACE = 100.0
+
+
+def cost(us):
+    return pl.CostEstimate(flops=int(us * PACE * 1.15e9), bytes_accessed=int(us * 3.0e6), transcendentals=0)
 
 
 def full(*shape):
@@ -44,41 +50,55 @@
     return jnp.sum(jnp.where(eye, row, 0), axis=1, keepdims=True)
 
 
-def route_kernel(m, owners, cap, ids_ref, table_ref, cot_ref, slot_ref, pack_ref):
-    n = ids_ref.shape[1]
-    ids = ids_ref[pl.ds(m, 1), :]
+def spread(slots, values, count):
+    total = None
+    for slot, value in zip(slots, values):
+        places = (iota((count, slot.shape[1]), 0) == slot).astype(BF16)
+        part = dot(places, value)
+        total = part if total is None else total + part
+    return total.astype(BF16)
+
+
+def route_kernel(owners, cap, ids_ref, table_ref, cot_ref, slot0_ref, slot1_ref, pack_ref):
+    micro, n = ids_ref.shape
     rows = table_ref.shape[0]
-    pick = (iota((rows, n), 0) == (ids >> 7)).astype(BF16)
-    values = dot(table_ref[...].astype(BF16), pick, 0, 0)
-    lane = ids & 127
-    expert = jnp.sum(jnp.where(iota((128, n), 0) == lane, values, 0.0), axis=0, keepdims=True)
+    table = table_ref[...].astype(BF16)
     kinds = -(-owners // 16) * 16
-    named = iota((kinds, n), 0).astype(F32) == expert
     before = (iota((n, n), 0) < iota((n, n), 1)).astype(BF16)
-    counts = dot(named.astype(BF16), before)
-    rank = jnp.sum(jnp.where(named, counts, 0.0), axis=0, keepdims=True)
-    slot = (expert * cap + rank).astype(jnp.int32)
-    slot_ref[...] = slot
-    places = (iota((owners * cap, n), 0) == slot).astype(BF16)
-    pack_ref[...] = dot(places, cot_ref[0]).astype(BF16)
-
-
-def route(m, ids, table, cot, owners, cap):
+    slots = []
+    for m, slot_ref in enumerate((slot0_ref, slot1_ref)):
+        ids = ids_ref[pl.ds(m, 1), :]
+        pick = (iota((rows, n), 0) == (ids >> 7)).astype(BF16)
+        values = dot(table, pick, 0, 0)
+        lane = ids & 127
+        expert = jnp.sum(
+            jnp.where(iota((128, n), 0) == lane, values, 0.0), axis=0, keepdims=True
+        )
+        named = iota((kinds, n), 0).astype(F32) == expert
+        counts = dot(named.astype(BF16), before)
+        rank = jnp.sum(jnp.where(named, counts, 0.0), axis=0, keepdims=True)
+        slot = (expert * cap + rank).astype(jnp.int32)
+        slot_ref[...] = slot
+        slots.append(slot)
+    pack_ref[...] = spread(slots[:1], (cot_ref[0],), pack_ref.shape[0])
+
+
+def route(ids, table, cot, owners, cap):
     micro, n = ids.shape
     width = cot.shape[2]
     rows = table.shape[0]
     return pl.pallas_call(
-        functools.partial(route_kernel, m, owners, cap),
+        functools.partial(route_kernel, owners, cap),
         grid=(1,),
-        in_specs=[
-            full(micro, n), full(rows, 128), pl.BlockSpec((1, n, width), lambda i: (m, 0, 0)),
-        ],
-        out_specs=[full(1, n), full(owners * cap, width)],
+        in_specs=[full(micro, n), full(rows, 128), full(1, n, width)],
+        out_specs=[full(1, n), full(1, n), full(owners * cap, width)],
         out_shape=[
+            jax.ShapeDtypeStruct((1, n), jnp.int32),
             jax.ShapeDtypeStruct((1, n), jnp.int32),
             jax.ShapeDtypeStruct((owners * cap, width), BF16),
         ],
-        compiler_params=params(1),
+        cost_estimate=cost(5.0),
+        compiler_params=params(12),
     )(ids, table, cot)
 
 
@@ -90,8 +110,8 @@
 
 
 def forward_kernel(
-    m, slot_ref, seg_ref, tok_ref, wq_ref, wk_ref, wv_ref, wo_ref, ga_ref, gf_ref, dep_ref,
-    normed_ref, q_ref, k_ref, v_ref, lse_ref, mixed_ref, hidden_ref, pack_ref, bias_ref,
+    m, cap, slot_ref, seg_ref, tok_ref, cot_ref, wq_ref, wk_ref, wv_ref, wo_ref, ga_ref, gf_ref,
+    dep_ref, normed_ref, q_ref, k_ref, v_ref, lse_ref, mixed_ref, hidden_ref, last_ref, bias_ref,
 ):
     x = tok_ref[0].astype(F32)
     n = x.shape[0]
@@ -125,101 +145,152 @@
     hidden_ref[...] = hidden
     r = lax.rsqrt(jnp.mean(hidden * hidden, axis=1, keepdims=True) + EPS)
     routed = (hidden * r * gf_ref[...]).astype(BF16)
-    places = (iota((pack_ref.shape[0], n), 0) == slot_ref[...]).astype(BF16)
-    pack_ref[...] = dot(places, routed).astype(BF16)
-
-
-def forward(m, slot, seg, tokens, wq, wk, wv, wo, ga, gf, slots, dep):
+    slot = slot_ref[...]
+    if m == 0:
+        last_ref[...] = spread((slot,), (routed,), last_ref.shape[0])
+    else:
+        slot = slot + slot // cap * cap
+        last_ref[...] = spread((slot, slot + cap), (cot_ref[0], routed), last_ref.shape[0])
+
+
+def forward(m, slot, seg, tokens, cot, wq, wk, wv, wo, ga, gf, slots, cap, dep):
     _, n, d = tokens.shape
     shapes = [
         ((n, d), BF16), ((n, d), BF16), ((n, d), BF16), ((n, d), BF16), ((16, n), F32),
-        ((n, d), BF16), ((n, d), F32), ((slots, d), BF16),
+        ((n, d), BF16), ((n, d), F32), ((slots * (m + 1), d), BF16),
     ]
-    return pl.pallas_call(
-        functools.partial(forward_kernel, m),
+    mat = pl.BlockSpec((1, n, d), lambda i: (m, 0, 0))
+    return pl.pallas_call(
+        functools.partial(forward_kernel, m, cap),
         grid=(1,),
         in_specs=[
-            full(1, n), full(*seg.shape), pl.BlockSpec((1, n, d), lambda i: (m, 0, 0)),
+            full(1, n), full(*seg.shape), mat, mat,
             full(d, d), full(d, d), full(d, d), full(d, d), full(1, d), full(1, d), ANY,
         ],
         out_specs=[full(*s) for s, _ in shapes],
         out_shape=[jax.ShapeDtypeStruct(s, t) for s, t in shapes],
         scratch_shapes=[pltpu.VMEM((n, n), F32)],
-        compiler_params=params(1),
-    )(slot, seg, tokens, wq, wk, wv, wo, ga, gf, dep)
+        cost_estimate=cost(13.4),
+        compiler_params=params(26),
+    )(slot, seg, tokens, cot, wq, wk, wv, wo, ga, gf, dep)
 
 
 BLOCK = 256
-
-
-def expert_kernel(rx0_ref, rx1_ref, g0_ref, g1_ref, win_ref, wout_ref, *rest):
-    chunk_ref, act_ref, gpre_ref = rest[-3:]
-    win, wout = win_ref[0], wout_ref[0]
-    f = win.shape[1]
-    rows = rx0_ref.shape[0]
-    gout, gin = None, None
-    for m, (x_ref, g_ref) in enumerate(((rx0_ref, g0_ref), (rx1_ref, g1_ref))):
-        x, g = x_ref[...], g_ref[...]
-        pre = dot(x, win)
-        sig = jax.nn.sigmoid(pre)
-        act = (pre * sig).astype(BF16)
-        slope = sig * (1.0 + pre * (1.0 - sig))
-        gpre = (dot(g, wout, 1, 1) * slope).astype(BF16)
-        act_ref[pl.ds(m * rows, rows), :] = act
-        gpre_ref[pl.ds(m * rows, rows), :] = gpre
-        a, b = dot(act, g, 0, 0), dot(gpre, x, 0, 0)
-        gout, gin = (a, b) if m == 0 else (gout + a, gin + b)
-    chunk_ref[pl.ds(0, f), :] = gout.astype(BF16)
-    chunk_ref[pl.ds(f, f), :] = gin.astype(BF16)
-
-
-def expert(c, units, rx, g, win, wout, held, dep):
-    rows, d = rx[0].shape
-    ff = win.shape[2]
+HALF = 128
+
+
+def hidden_units(x, g, win, wout):
+    pre = dot(x, win)
+    sig = jax.nn.sigmoid(pre)
+    soft = pre * sig
+    slope = sig + soft * (1.0 - sig)
+    return soft.astype(BF16), (dot(g, wout, 1, 1) * slope).astype(BF16)
+
+
+def put_chunk(chunk_ref, gout, gin):
+    for i in range(BLOCK // HALF):
+        part = slice(i * HALF, (i + 1) * HALF)
+        chunk_ref[pl.ds(2 * i * HALF, HALF), :] = gout[part].astype(BF16)
+        chunk_ref[pl.ds((2 * i + 1) * HALF, HALF), :] = gin[part].astype(BF16)
+
+
+def units_kernel(rx_ref, gx_ref, win_ref, wout_ref, *rest):
+    act_ref, gpre_ref = rest[-2:]
+    act_ref[...], gpre_ref[...] = hidden_units(
+        rx_ref[...], gx_ref[...], win_ref[0], wout_ref[0]
+    )
+
+
+def split_units_kernel(cap, both_ref, win_ref, wout_ref, *rest):
+    act_ref, gpre_ref, rx_ref, gx_ref = rest[-4:]
+
+    @pl.when(pl.program_id(0) == 0)
+    def _():
+        for e in range(rx_ref.shape[0] // cap):
+            mine = pl.ds(e * cap, cap)
+            gx_ref[mine, :] = both_ref[pl.ds(2 * e * cap, cap), :]
+            rx_ref[mine, :] = both_ref[pl.ds((2 * e + 1) * cap, cap), :]
+
+    act_ref[...], gpre_ref[...] = hidden_units(
+        rx_ref[...], gx_ref[...], win_ref[0], wout_ref[0]
+    )
+
+
+def expert_units(c, units, given, win, wout, dep, cap=None):
+    d = win.shape[1]
+    rows = given[0].shape[0] // (1 if cap is None else 2)
     f = BLOCK
-    extra = ([] if held is None else list(held)) + [dep]
-    alias = {} if held is None else {6: 1, 7: 2}
-    return pl.pallas_call(
-        expert_kernel,
+    columns = pl.BlockSpec((rows, f), lambda i: (0, i))
+    kernel = units_kernel if cap is None else functools.partial(split_units_kernel, cap)
+    return pl.pallas_call(
+        kernel,
         grid=(units,),
-        in_specs=[full(rows, d)] * 4
+        in_specs=[full(*x.shape) for x in given]
         + [
             pl.BlockSpec((1, d, f), lambda i: (0, 0, c + i)),
             pl.BlockSpec((1, f, d), lambda i: (0, c + i, 0)),
-        ]
-        + [ANY] * len(extra),
-        out_specs=[
-            pl.BlockSpec((2 * f, d), lambda i: (i, 0)),
-            pl.BlockSpec((2 * rows, f), lambda i: (0, c + i)),
-            pl.BlockSpec((2 * rows, f), lambda i: (0, c + i)),
+            ANY,
         ],
-        out_shape=[
-            jax.ShapeDtypeStruct((units * 2 * f, d), BF16),
-            jax.ShapeDtypeStruct((2 * rows, ff), BF16),
-            jax.ShapeDtypeStruct((2 * rows, ff), BF16),
-        ],
-        input_output_aliases=alias,
-        compiler_params=params(1),
-    )(*rx, *g, win, wout, *extra)
-
-
-def rows_kernel(side, a_ref, w_ref, dep_ref, o_ref):
-    o_ref[...] = dot(a_ref[...], w_ref[0], 1, side).astype(BF16)
-
-
-def back_rows(m, a, w, side, dep, blk=384):
-    ff = a.shape[1]
-    rows = a.shape[0] // 2
+        out_specs=[columns] * 2 + ([full(rows, d)] * 2 if cap else []),
+        out_shape=[jax.ShapeDtypeStruct((rows, units * f), BF16)] * 2
+        + ([jax.ShapeDtypeStruct((rows, d), BF16)] * 2 if cap else []),
+        cost_estimate=cost(3 + units),
+        compiler_params=params(20),
+    )(*given, win, wout, dep)
+
+
+def chunk_kernel(
+    rx0_ref, rx1_ref, gx0_ref, gx1_ref, act0_ref, act1_ref, gpre0_ref, gpre1_ref, dep_ref,
+    chunk_ref,
+):
+    put_chunk(
+        chunk_ref,
+        dot(act0_ref[...], gx0_ref[...], 0, 0) + dot(act1_ref[...], gx1_ref[...], 0, 0),
+        dot(gpre0_ref[...], rx0_ref[...], 0, 0) + dot(gpre1_ref[...], rx1_ref[...], 0, 0),
+    )
+
+
+def expert_grads(units, rx, gx, acts, gpres, at, dep):
+    rows, d = rx[0].shape
+    f = BLOCK
+    columns = [pl.BlockSpec((rows, f), lambda i, k=k: (0, k + i)) for k in at]
+    return pl.pallas_call(
+        chunk_kernel,
+        grid=(units,),
+        in_specs=[full(rows, d)] * 4 + columns * 2 + [ANY],
+        out_specs=pl.BlockSpec((2 * f, d), lambda i: (i, 0)),
+        out_shape=jax.ShapeDtypeStruct((units * 2 * f, d), BF16),
+        cost_estimate=cost(0.5 + 1.5 * units),
+        compiler_params=params(20),
+    )(*rx, *gx, *acts, *gpres, dep)
+
+
+def rows_kernel(side, *refs):
+    *parts, w_ref, _, o_ref = refs
+    total, start = None, 0
+    for a_ref in parts:
+        count = a_ref.shape[1]
+        units = pl.ds(start, count)
+        w = w_ref[0, :, units] if side == 1 else w_ref[0, units, :]
+        term = dot(a_ref[...], w, 1, side)
+        total = term if total is None else total + term
+        start += count
+    o_ref[...] = total.astype(BF16)
+
+
+def back_rows(parts, w, side, dep, blk=256):
+    rows = parts[0].shape[0]
     d = w.shape[1 + (1 - side)]
-    steps = rows // blk
     return pl.pallas_call(
         functools.partial(rows_kernel, side),
-        grid=(steps,),
-        in_specs=[pl.BlockSpec((blk, ff), lambda i: (m * steps + i, 0)), full(*w.shape), ANY],
+        grid=(rows // blk,),
+        in_specs=[pl.BlockSpec((blk, a.shape[1]), lambda i: (i, 0)) for a in parts]
+        + [full(*w.shape), ANY],
         out_specs=pl.BlockSpec((blk, d), lambda i: (i, 0)),
         out_shape=jax.ShapeDtypeStruct((rows, d), BF16),
-        compiler_params=params(1),
-    )(a, w, dep)
+        cost_estimate=cost(4.5),
+        compiler_params=params(16),
+    )(*parts, w, dep)
 
 
 def backward_kernel(
@@ -299,7 +370,8 @@
         scratch_shapes=[
             pltpu.VMEM((n, n), F32), pltpu.VMEM((n, d), BF16), pltpu.VMEM((n, d), F32)
         ],
-        compiler_params=params(1),
+        cost_estimate=cost(17.5),
+        compiler_params=params(36),
         input_output_aliases={} if held is None else {18: 0},
     )(slot, seg, tokens, cot, back, normed, q, k, v, lse, hidden, wq, wk, wv, wo, ga, gf, *extra)
 
@@ -330,7 +402,8 @@
         in_specs=[full(*a.shape) for a in flat] + [ANY],
         out_specs=full(4 * d + rest, d),
         out_shape=jax.ShapeDtypeStruct((4 * d + rest, d), BF16),
-        compiler_params=params(1),
+        cost_estimate=cost(10.3),
+        compiler_params=params(36),
     )(*flat, dep)
 
 
@@ -351,50 +424,26 @@
         in_specs=[full(*a.shape) for a in flat] + [ANY],
         out_specs=full(micro, n, d),
         out_shape=jax.ShapeDtypeStruct((micro, n, d), BF16),
-        compiler_params=params(1),
+        cost_estimate=cost(4.4),
+        compiler_params=params(16),
     )(*flat, dep)
 
 
-def add_kernel(a_ref, b_ref, dep_ref, o_ref):
-    o_ref[...] = (a_ref[...].astype(F32) + b_ref[...].astype(F32)).astype(BF16)
+def after(x, dep):
+    return lax.optimization_barrier((x, dep))[0]
 
 
 def add(a, b, dep):
-    rows, d = a.shape
-    blk = 2 * BLOCK if rows % (2 * BLOCK) == 0 else rows
-    spec = pl.BlockSpec((blk, d), lambda i: (i, 0))
-    return pl.pallas_call(
-        add_kernel,
-        grid=(rows // blk,),
-        in_specs=[spec, spec, ANY],
-        out_specs=spec,
-        out_shape=jax.ShapeDtypeStruct((rows, d), BF16),
-        compiler_params=params(1),
-    )(a, b, dep)
-
-
-def pick_kernel(flag_ref, a_ref, b_ref, dep_ref, o_ref):
-    o_ref[...] = jnp.where(flag_ref[0] == 1, b_ref[...], a_ref[...])
-
-
-def pick(flag, a, b, dep):
-    return pl.pallas_call(
-        pick_kernel,
-        in_specs=[pl.BlockSpec(memory_space=pltpu.SMEM)]
-        + [pl.BlockSpec(memory_space=pltpu.VMEM)] * 2 + [ANY],
-        out_specs=pl.BlockSpec(memory_space=pltpu.VMEM),
-        out_shape=jax.ShapeDtypeStruct(a.shape, BF16),
-        compiler_params=params(0),
-    )(flag, a, b, dep)
+    return (after(a, dep).astype(F32) + b.astype(F32)).astype(BF16)
 
 
 def store_kernel(flag_ref, a_ref, b_ref, *rest):
-    gin_ref, gout_ref = rest[-2:]
-    f = gout_ref.shape[1]
+    gin_ref, gout_ref, token_ref = rest[-3:]
+    token_ref[...] = jnp.zeros_like(token_ref)
 
     def put(ref):
-        gout_ref[0] = ref[pl.ds(0, f), :].astype(F32)
-        gin_ref[0] = ref[pl.ds(f, f), :].astype(F32).T
+        gout_ref[0] = ref[pl.ds(0, HALF), :].astype(F32)
+        gin_ref[0] = ref[pl.ds(HALF, HALF), :].astype(F32).T
 
     @pl.when(flag_ref[0] == 1)
     def _():
@@ -407,36 +456,42 @@
 
 def store(c, flag, a, b, ff, held, dep):
     rows, d = a.shape
-    f = BLOCK
-    spec = pl.BlockSpec((2 * f, d), lambda i: (i, 0))
+    spec = pl.BlockSpec((2 * HALF, d), lambda i: (i, 0))
+    base = c * (BLOCK // HALF)
     extra = ([] if held is None else list(held)) + [dep]
     return pl.pallas_call(
         store_kernel,
-        grid=(rows // (2 * f),),
+        grid=(rows // (2 * HALF),),
         in_specs=[pl.BlockSpec(memory_space=pltpu.SMEM), spec, spec] + [ANY] * len(extra),
         out_specs=[
-            pl.BlockSpec((1, d, f), lambda i: (0, 0, c + i)),
-            pl.BlockSpec((1, f, d), lambda i: (0, c + i, 0)),
+            pl.BlockSpec((1, d, HALF), lambda i: (0, 0, base + i)),
+            pl.BlockSpec((1, HALF, d), lambda i: (0, base + i, 0)),
+            full(8, 128),
         ],
         out_shape=[
             jax.ShapeDtypeStruct((1, d, ff), F32),
             jax.ShapeDtypeStruct((1, ff, d), F32),
+            jax.ShapeDtypeStruct((8, 128), F32),
         ],
         input_output_aliases={} if held is None else {3: 0, 4: 1},
-        compiler_params=params(1),
+        cost_estimate=cost(0.8 + rows / 480),
+        compiler_params=params(6),
     )(flag, a, b, *extra)
 
 
-SIZES = (1, 1, 2, 2, 2, 2, 1, 1)
+SIZES = (1, 1, 1, 1, 1, 1, 1, 1, 1, 1, 1, 1)
 
 
 PLAN = (
-    ("E", 0), ("S1", 0), ("E", 1), ("S1", 1), ("E", 2), ("E", 3), ("S1", 2), ("G1", 0), ("E", 4),
-    ("S1", 3), ("G1", 1), ("E", 5), ("G2", 0), ("E", 6), ("E", 7), ("G2", 1), ("Q1", 0), ("G3", 0),
-    ("Q1", 1), ("G3", 1), ("S1", 4), ("G1", 2), ("B", 0), ("S1", 5), ("G1", 3), ("B", 1), ("W", 0),
-    ("G2", 2), ("Q2", 0), ("S1", 6), ("G1", 4), ("Q2", 1), ("G2", 3), ("S1", 7), ("G1", 5), ("O",
-    0), ("G3", 2), ("G1", 6), ("S1", "A"), ("G1", 7), ("G1", "A"), ("G3", 3), ("G2", 4), ("G2", 6),
-    ("G3", 4), ("G2", "A"), ("G2", 7), ("G2", 5), ("G3", 6), ("G3", "A"), ("G3", 7), ("G3", 5),
+    ("F", 0), ("Q1", 0), ("Fa", 1), ("D", 0), ("S1", 0), ("Fb", 1), ("D", 1), ("S1", 1), ("D", 2),
+    ("D", 3), ("G1", 0), ("Q1", 1), ("S1", 2), ("D", 4), ("G1", 1), ("D", 5), ("S1", 3), ("G2", 0),
+    ("B", 0), ("G1", 2), ("G2", 1), ("S1", 4), ("G1", 3), ("B", 1), ("S1", 5), ("G2", 2), ("G1", 4),
+    ("W", 0), ("D", 6), ("G2", 3), ("S1", 6), ("G1", 5), ("G2", 4), ("D", 7), ("S1", 7), ("D", 8),
+    ("G3", 0), ("G1", 6), ("G2", 5), ("G1", 7), ("S1", 8), ("G2", 6), ("D", 9), ("S1", 9), ("D",
+    10), ("A2", 0), ("G3", 1), ("G2", 7), ("G1", 8), ("Q2", 1), ("S1", 10), ("G3", 2), ("G1", 9),
+    ("G2", 8), ("D", 11), ("G3", 3), ("G3", 4), ("G1", 10), ("S1", 11), ("G3", 5), ("G2", 9), ("G3",
+    6), ("G3", 7), ("A3", 0), ("G1", 11), ("G2", 10), ("Q2", 0), ("G2", 11), ("O", 0), ("G3", 8),
+    ("G3", 9), ("G3", 10), ("G3", 11),
 )
 
 
@@ -460,40 +515,48 @@
     def swap(x):
         return lax.all_to_all(x, "expert", split_axis=0, concat_axis=0, tiled=True)
 
-    def after(x, dep):
-        return lax.optimization_barrier((x, dep))[0]
-
-    slots, saved, rx, gx = [], [], [], []
-    dep = None
-    for m in range(micro):
-        slot, packed = route(m, token_ids, table, cotangent, owners, cap)
-        gx.append(swap(packed))
-        dep = packed if dep is None else dep
-        *kept, packed = forward(
-            m, slot, segment_ids, tokens, *weights, *gains, owners * cap, dep
-        )
-        rx.append(swap(packed))
-        dep = packed
-        slots.append(slot)
-        saved.append(tuple(kept))
+    slot0, slot1, packed = route(token_ids, table, cotangent, owners, cap)
+    slots = (slot0, slot1)
+    gx = {0: swap(packed)}
+    *kept0, packed0 = forward(
+        0, slot0, segment_ids, tokens, cotangent, *weights, *gains, owners * cap, cap, packed
+    )
+    rx = {0: swap(after(packed0, gx[0]))}
+    *kept1, packed1 = forward(
+        1, slot1, segment_ids, tokens, cotangent, *weights, *gains, owners * cap, cap, packed0
+    )
+    both = swap(after(packed1, rx[0]))
+    saved = (tuple(kept0), tuple(kept1))
+    dep = packed1
 
     starts = [sum(SIZES[:i]) for i in range(len(SIZES))]
     chunk, hop1, hop2, hop3, sum1, total = {}, {}, {}, {}, {}, {}
-    held = stored = gtok = None
+    stored = gtok = dense = block_out = None
     backs, results, grads = {}, {}, {}
-    dense = block_out = None
     for op, c in PLAN:
-        if op == "E":
-            chunk[c], *held = expert(
-                starts[c], SIZES[c], rx, gx, expert_in, expert_out, held, dep
+        if op == "F":
+            act0, gpre0 = expert_units(0, ff // BLOCK, (rx[0], gx[0]), expert_in, expert_out, dep)
+            dep = act0
+        elif op == "Fa":
+            acta, gprea, rx[1], gx[1] = expert_units(
+                0, SIZES[0], (both,), expert_in, expert_out, dep, cap
             )
-            dep = chunk[c]
+            dep = rx[1]
+        elif op == "Fb":
+            actb, gpreb = expert_units(
+                SIZES[0], ff // BLOCK - SIZES[0], (rx[1], gx[1]), expert_in, expert_out, dep
+            )
+            dep = actb
+        elif op == "D":
+            mine = (acta, gprea) if c == 0 else (actb, gpreb)
+            at = (starts[c], 0 if c == 0 else starts[c] - SIZES[0])
+            dep = chunk[c] = expert_grads(
+                SIZES[c], (rx[0], rx[1]), (gx[0], gx[1]), (act0, mine[0]), (gpre0, mine[1]), at,
+                dep,
+            )
         elif op == "S1":
             x = after(chunk[c], dep)
-            if depth == 4:
-                hop1[c] = lax.ppermute(x, "dp", [(0, 1), (3, 2)])
-            else:
-                hop1[c] = x
+            hop1[c] = lax.ppermute(x, "dp", [(0, 1), (3, 2)]) if depth == 4 else x
         elif op == "G1":
             if depth == 4:
                 sum1[c] = add(chunk[c], hop1[c], dep)
@@ -507,18 +570,12 @@
             else:
                 total[c] = hop3[c] = lax.psum(hop1[c], "dp")
         elif op == "G3":
-            if c == "A":
-                dense = pick(outer, total[c], hop3[c], dep)
-                dep = dense
-                dense = lax.all_gather(dense, "expert", axis=0, tiled=True)
-            else:
-                stored = store(starts[c], outer, total[c], hop3[c], ff, stored, dep)
-                dep = stored[0]
+            *stored, dep = store(starts[c], outer, total[c], hop3[c], ff, stored, dep)
         elif op == "Q1":
-            dep = back_rows(c, held[1], expert_in, 1, dep)
+            dep = back_rows((gpre0,) if c == 0 else (gprea, gpreb), expert_in, 1, dep)
             backs[c] = swap(dep)
         elif op == "Q2":
-            dep = back_rows(c, held[0], expert_out, 0, dep)
+            dep = back_rows((act0,) if c == 0 else (acta, actb), expert_out, 0, dep)
             results[c] = swap(dep)
         elif op == "B":
             gtok, *grads[c] = backward(
@@ -528,7 +585,11 @@
             dep = grads[c][0]
         elif op == "W":
             dep = dense_grads(saved, grads, 16 * owners, dep)
-            chunk["A"] = lax.psum_scatter(dep, "expert", scatter_dimension=0, tiled=True)
+            dense = lax.psum_scatter(dep, "expert", scatter_dimension=0, tiled=True)
+        elif op == "A2":
+            dense = lax.psum(after(dense, dep), "dp")
+        elif op == "A3":
+            dense = lax.all_gather(after(dense, dep), "expert", axis=0, tiled=True)
         elif op == "O":
             block_out = block_output(
                 slots, [results[m] for m in range(micro)], [s[6] for s in saved], dep

time: 690 us -> 691 us (level)
  blocking collectives: 82.1 us -> 0 us
  local copies, waits for them, and re-layouts: 33.3 us -> 107 us
  Pallas kernels: 251 us -> 186 us
  other arithmetic: 3.31 us -> 63.2 us
  starting transfers between devices: 101 us -> 143 us
  waiting for transfers between devices: 194 us -> 164 us
    ppermute x9 -> x12, waiting for transfers between devices: 152 us -> 21.2 us  [per_device(): hop3[c] = lax.ppermute(total[c], 'dp', [(1, 0), (2, 3)])]
    all_to_all x4 -> x0, blocking collectives: 82.1 us -> none  [swap(): return lax.all_to_all(x, 'expert', split_axis=0, concat_axis=0, tiled=True)]
    unnamed x75 -> x228, local copies, waits for them, and re-layouts: 26.3 us -> 102 us
    convert_element_type x0 -> x24, other arithmetic: none -> 59.9 us  [add(): return (after(a, dep).astype(F32) + b.astype(F32)).astype(BF16)]
    pallas_call x43 -> x34, Pallas kernels: 201 us -> 148 us  [the longest x12 46.8 us: expert_grads(): pl.pallas_call(chunk_kernel, grid=(units,), in_specs=[full(rows, d)] * 4...]
    psum x0 -> x1, waiting for transfers between devices: none -> 42.2 us  [per_device(): dense = lax.psum(after(dense, dep), 'dp')]
    all_gather x1, waiting for transfers between devices: 0.01 us -> 39.1 us  [per_device(): dense = lax.all_gather(after(dense, dep), 'expert', axis=0, tiled=True)]
    all_to_all x4 -> x7, starting transfers between devices: 16.1 us -> 30.7 us  [swap(): return lax.all_to_all(x, 'expert', split_axis=0, concat_axis=0, tiled=True)]
  transfers between devices with their start and end apart: 33 -> 46, of which waited for: 10 -> 12; matrix products, arithmetic and copies ran while one was open for 1% -> 9% of each run, Pallas kernels for 25% -> 27%
where the time goes in v2:
time: 691 us; the launch traced here: 679 us
  Pallas kernels  186 us (27%)
  waiting for transfers between devices  164 us (24%)
  starting transfers between devices  143 us (21%)
  local copies, waits for them, and re-layouts  107 us (15%)
  other arithmetic  63.2 us (9%)
  between operations  15 us (2%)
    unnamed x228, local copies, waits for them, and re-layouts  102 us
    ppermute x12, starting transfers between devices, per_device(): hop1[c] = lax.ppermute(x, 'dp', [(0, 1), (3, 2)]) if depth == 4 else x  76.9 us
    convert_element_type x24, other arithmetic, add(): return (after(a, dep).astype(F32) + b.astype(F32)).astype(BF16)  59.9 us
    pallas_call x12, Pallas kernels, expert_grads(): pl.pallas_call(chunk_kernel, grid=(units,), in_specs=[full(rows, d)] * 4...  46.8 us
    psum x1, waiting for transfers between devices, per_device(): dense = lax.psum(after(dense, dep), 'dp')  42.2 us
    all_gather x1, waiting for transfers between devices, per_device(): dense = lax.all_gather(after(dense, dep), 'expert', axis=0, tiled=True)  39.1 us
    ppermute x12, waiting for transfers between devices, per_device(): hop1[c] = lax.ppermute(x, 'dp', [(0, 1), (3, 2)]) if depth == 4 else x  37.1 us
    all_to_all x7, starting transfers between devices, swap(): return lax.all_to_all(x, 'expert', split_axis=0, concat_axis=0, tiled=True)  30.7 us
  transfers between devices with their start and end apart: 46, of which 12 were waited for; matrix products, arithmetic and copies ran while one was open for 9% of the time, Pallas kernels for 27%

profile of v2, /device:TPU:0, one launch (start us, length us, event | category | flops | bytes accessed | tf_op | source)
XLA Modules:
  0.0 678.7 jit_solution(4138533655770739239)
XLA Ops:
  12.7 5.3 all-to-all-start
  23.8 10.8 %shard_map.205 = (bf16[384,768]{1,0:T(8,128)(2,1)S(1)}, bf16[384,768]{1,0:T(8,128)(2,1)S(1)}, bf16[384,768]{1,0:T(8,128)(2,1)S(1)}, bf16[384,768]{1,0:T(8,128)(2...) custom-call(s32[1,384]{1,0:T(1,128)S(1)} %get-tuple-element.114.slot, ...), custom_call_target="tpu_custom_call" | custom-call | flops 1541000003584 | bytes 40200000 | tf_op jit(solution)/shard_map/pallas_call | solution.py:163
  40.5 4.4 all-to-all-start.1
  49.5 13.0 %shard_map.206 = (bf16[384,768]{1,0:T(8,128)(2,1)S(1)}, bf16[384,768]{1,0:T(8,128)(2,1)S(1)}, bf16[384,768]{1,0:T(8,128)(2,1)S(1)}, bf16[384,768]{1,0:T(8,128)(2...) custom-call(s32[1,384]{1,0:T(1,128)S(1)} %copy-done.109, ...), custom_call_target="tpu_custom_call" | custom-call | flops 1541000003584 | bytes 40200000 | tf_op jit(solution)/shard_map/pallas_call | solution.py:163
  68.3 4.6 all-to-all-start.2
  77.6 13.3 %shard_map.207 = (bf16[768,3072]{1,0:T(8,128)(2,1)S(1)}, bf16[768,3072]{1,0:T(8,128)(2,1)S(1)}) custom-call(bf16[768,768]{1,0:T(8,128)(2,1)} %bitcast.4.rx_ref.rx0_ref, bf16[768,768]{1,0:T(8,128)(2,1)} %bitcast.2.gx_ref.gx0_ref, bf16[1,768,3072]{2,1,0:T(8,128)(2,1)S(1)} %copy-done.4, bf16[1,3072,768]{2,1,0:T(8,128)(2,1)S(1)} %copy-done.9, ...), custom_call_target="tpu_custom_call" | custom-call | flops 1725000056832 | bytes 45000000 | tf_op jit(solution)/shard_map/pallas_call | solution.py:225
  90.9 5.0 shard_map.208.rest_0_
  121.5 10.3 %shard_map.211 = (bf16[768,2816]{1,0:T(8,128)(2,1)S(1)}, bf16[768,2816]{1,0:T(8,128)(2,1)S(1)}) custom-call(bf16[768,768]{1,0:T(8,128)(2,1)S(1)} %get-tuple-element.123.rx1_ref.dep_ref.rx_ref, bf16[768,768]{1,0:T(8,128)(2,1)S(1)} %get-tuple-element.124.gx1_ref.gx_ref, bf16[1,768,3072]{2,1,0:T(8,128)(2,1)S(1)} %copy-done.7, ...), custom_call_target="tpu_custom_call" | custom-call | flops 1609999974400 | bytes 42000000 | tf_op jit(solution)/shard_map/pallas_call | solution.py:225
  131.8 4.9 collective-permute-start
  158.8 5.0 shard_map.215.dep_ref
  178.1 7.6 %collective-permute-start.3 = (bf16[512,768]{1,0:T(8,128)(2,1)}, bf16[512,768]{1,0:T(8,128)(2,1)}, u32[]{:S(2)}, u32[]{:S(2)}) collective-permute-start(bf16[512,768]{1,0:T(8,128)(2,1)} %shard_map.213.dep_ref), channel_id=1, source_target_pairs={{0,8},{24,16},{1,9},{25,17},{2,10},{26,18},{3,11},{27,19},{4,12},{... | collective-permute-start | bytes 2359304 | tf_op jit(solution)/shard_map/ppermute | solution.py:559
  204.6 14.6 %shard_map.218 = (bf16[2,384,768]{2,1,0:T(8,128)(2,1)}, bf16[384,768]{1,0:T(8,128)(2,1)S(1)}, bf16[384,768]{1,0:T(8,128)(2,1)S(1)}, bf16[384,768]{1,0:T(8,128)(2...) custom-call(s32[1,384]{1,0:T(1,128)S(1)} %get-tuple-element.114.slot_ref.s0_ref, s32[2,384]{1,0:T(2,128)S(1)} %copy-done.32, ...), custom_call_target="tpu_custom_call" | custom-call | flops 2012499935232 | bytes 52500000 | tf_op jit(solution)/shard_map/pallas_call | solution.py:360
  233.2 9.3 %collective-permute-start.7 = (bf16[512,768]{1,0:T(8,128)(2,1)}, bf16[512,768]{1,0:T(8,128)(2,1)}, u32[]{:S(2)}, u32[]{:S(2)}) collective-permute-start(bf16[512,768]{1,0:T(8,128)(2,1)} %shard_map.216), channel_id=1, source_target_pairs={{0,8},{24,16},{1,9},{25,17},{2,10},{26,18},{3,11},{27,19},{4,12},{... | collective-permute-start | bytes 2359304 | tf_op jit(solution)/shard_map/ppermute | solution.py:559
  253.2 14.7 %shard_map.219 = (bf16[2,384,768]{2,1,0:T(8,128)(2,1)}, bf16[384,768]{1,0:T(8,128)(2,1)S(1)}, bf16[384,768]{1,0:T(8,128)(2,1)S(1)}, bf16[384,768]{1,0:T(8,128)(2...) custom-call(s32[1,384]{1,0:T(1,128)S(1)} %copy-done.110, ...), custom_call_target="tpu_custom_call", output_to_operand_aliasing={{0}: (18, {})} | custom-call | flops 2012499935232 | bytes 52500000 | tf_op jit(solution)/shard_map/pallas_call | solution.py:360
  277.7 5.1 shard_map.220.dep_ref
  304.4 6.3 collective-permute-start.9
  346.2 8.9 %collective-permute-done.13 = bf16[512,768]{1,0:T(8,128)(2,1)} collective-permute-done((bf16[512,768]{1,0:T(8,128)(2,1)}, bf16[512,768]{1,0:T(8,128)(2,1)}, u32[]{:S(2)}, u32[]{:S(2)}) %collective-permute-start.13) | collective-permute-done | bytes 786464 | tf_op jit(solution)/shard_map/ppermute | solution.py:559
  370.7 7.7 %collective-permute-start.16 = (bf16[512,768]{1,0:T(8,128)(2,1)}, bf16[512,768]{1,0:T(8,128)(2,1)}, u32[]{:S(2)}, u32[]{:S(2)}) collective-permute-start(bf16[512,768]{1,0:T(8,128)(2,1)} %shard_map.225.rest_0_), channel_id=1, source_target_pairs={{0,8},{24,16},{1,9},{25,17},{2,10},{26,18},{3,11},{27,19},{4,12},{... | collective-permute-start | bytes 2359304 | tf_op jit(solution)/shard_map/ppermute | solution.py:559
  384.7 7.4 %collective-permute-done.16 = bf16[512,768]{1,0:T(8,128)(2,1)} collective-permute-done((bf16[512,768]{1,0:T(8,128)(2,1)}, bf16[512,768]{1,0:T(8,128)(2,1)}, u32[]{:S(2)}, u32[]{:S(2)}) %collective-permute-start.16) | collective-permute-done | bytes 786464 | tf_op jit(solution)/shard_map/ppermute | solution.py:559
  392.1 5.3 collective-permute-start.18
  402.2 4.9 shard_map.226.rest_2_
  407.1 4.3 all-to-all-start.6
  434.1 16.8 %collective-permute-start.17 = (bf16[512,768]{1,0:T(8,128)(2,1)}, bf16[512,768]{1,0:T(8,128)(2,1)}, u32[]{:S(2)}, u32[]{:S(2)}) collective-permute-start(bf16[512,768]{1,0:T(8,128)(2,1)} %shard_map.224.rest_2_), channel_id=1, source_target_pairs={{0,8},{24,16},{1,9},{25,17},{2,10},{26,18},{3,11},{27,19},{4,12},{... | collective-permute-start | bytes 2359304 | tf_op jit(solution)/shard_map/ppermute | solution.py:559
  453.2 13.2 %collective-permute-done.17 = bf16[512,768]{1,0:T(8,128)(2,1)} collective-permute-done((bf16[512,768]{1,0:T(8,128)(2,1)}, bf16[512,768]{1,0:T(8,128)(2,1)}, u32[]{:S(2)}, u32[]{:S(2)}) %collective-permute-start.17) | collective-permute-done | bytes 786464 | tf_op jit(solution)/shard_map/ppermute | solution.py:559
  474.4 7.8 %collective-permute-start.29 = (bf16[512,768]{1,0:T(8,128)(2,1)}, bf16[512,768]{1,0:T(8,128)(2,1)}, u32[]{:S(2)}, u32[]{:S(2)}) collective-permute-start(bf16[512,768]{1,0:T(8,128)(2,1)} %shard_map.227.rest_2_), channel_id=1, source_target_pairs={{0,8},{24,16},{1,9},{25,17},{2,10},{26,18},{3,11},{27,19},{4,12},{... | collective-permute-start | bytes 2359304 | tf_op jit(solution)/shard_map/ppermute | solution.py:559
  491.8 4.6 collective-permute-done.29
  507.6 5.0 shard_map.236
  524.8 8.2 %all-to-all-done.5 = bf16[8,96,768]{2,1,0:T(8,128)(2,1)S(1)} async-done(((bf16[8,96,768]{2,1,0:T(8,128)(2,1)}), bf16[8,96,768]{2,1,0:T(8,128)(2,1)S(1)}, u32[]{:S(2)}, u32[]{:S(2)}) %all-to-all-start.5) | async-done | bytes 1179680 | tf_op jit(solution)/shard_map/all_to_all | solution.py:516
  536.6 21.1 %collective-permute-done.35.b_ref = bf16[512,768]{1,0:T(8,128)(2,1)} collective-permute-done((bf16[512,768]{1,0:T(8,128)(2,1)}, bf16[512,768]{1,0:T(8,128)(2,1)}, u32[]{:S(2)}, u32[]{:S(2)}) %collective-permute-start.35) | collective-permute-done | bytes 786464 | tf_op jit(solution)/shard_map/ppermute | solution.py:568
  563.9 13.9 %reduce-scatter.2.cloned.1.call-done = bf16[400,768]{1,0:T(8,128)(2,1)} async-done(((bf16[3200,768]{1,0:T(8,128)(2,1)}), bf16[400,768]{1,0:T(8,128)(2,1)}) %reduce-scatter.2.cloned.1.call-update) | async-done | bytes 614416 | tf_op jit(solution)/shard_map/reduce_scatter | solution.py:588
  580.3 42.2 %all-reduce.3.cloned.1.call-done = bf16[400,768]{1,0:T(8,128)(2,1)} async-done(((bf16[400,768]{1,0:T(8,128)(2,1)}), bf16[400,768]{1,0:T(8,128)(2,1)}) %all-reduce.3.cloned.1.call-update) | async-done | bytes 614416 | tf_op jit(solution)/shard_map/psum | solution.py:590
  624.9 39.1 %all-gather.2.cloned.1.call-done = bf16[3200,768]{1,0:T(8,128)(2,1)} async-done(((bf16[400,768]{1,0:T(8,128)(2,1)}), bf16[3200,768]{1,0:T(8,128)(2,1)}) %all-gather.2.cloned.1.call-update) | async-done | bytes 4915216 | tf_op jit(solution)/shard_map/all_gather | solution.py:592
  (359 shorter events, 319.2 us)
Async XLA Ops:
  12.7 27.9 %all-to-all-start = ((bf16[8,96,768]{2,1,0:T(8,128)(2,1)}), bf16[8,96,768]{2,1,0:T(8,128)(2,1)}, u32[]{:S(2)}, u32[]{:S(2)}) async-start(bf16[8,96,768]{2,1,0:T(8,128)(2,1)} %bitcast.1), calls=%async_computation | async-start | bytes 2359296 | tf_op jit(solution)/shard_map/all_to_all | solution.py:516
  40.5 27.7 %all-to-all-start.1 = ((bf16[8,96,768]{2,1,0:T(8,128)(2,1)}), bf16[8,96,768]{2,1,0:T(8,128)(2,1)}, u32[]{:S(2)}, u32[]{:S(2)}) async-start(bf16[8,96,768]{2,1,0:T(8,128)(2,1)} %bitcast.3), calls=%async_computation.1 | async-start | bytes 2359296 | tf_op jit(solution)/shard_map/all_to_all | solution.py:516
  68.3 34.1 %all-to-all-start.2 = ((bf16[8,192,768]{2,1,0:T(8,128)(2,1)}), bf16[8,192,768]{2,1,0:T(8,128)(2,1)}, u32[]{:S(2)}, u32[]{:S(2)}) async-start(bf16[8,192,768]{2,1,0:T(8,128)(2,1)} %bitcast.5), calls=%async_computation.2 | async-start | bytes 4718592 | tf_op jit(solution)/shard_map/all_to_all | solution.py:516
  102.4 87.9 %all-to-all-start.3 = ((bf16[8,96,768]{2,1,0:T(8,128)(2,1)}), bf16[8,96,768]{2,1,0:T(8,128)(2,1)}, u32[]{:S(2)}, u32[]{:S(2)}) async-start(bf16[8,96,768]{2,1,0:T(8,128)(2,1)} %bitcast.7), calls=%async_computation.3 | async-start | bytes 2359296 | tf_op jit(solution)/shard_map/all_to_all | solution.py:516
  176.6 48.8 %collective-permute-start.4 = (bf16[512,768]{1,0:T(8,128)(2,1)}, bf16[512,768]{1,0:T(8,128)(2,1)}, u32[]{:S(2)}, u32[]{:S(2)}) collective-permute-start(bf16[512,768]{1,0:T(8,128)(2,1)} %add_convert_fusion.22.dep_ref), channel_id=1, source_target_pairs={{8,16},{16,8},{9,17},{17,9},{10,18},{18,10},{11,19},{19,11},{12,20... | collective-permute-start | bytes 2359304 | tf_op jit(solution)/shard_map/ppermute | solution.py:563
  178.1 41.1 %collective-permute-start.3 = (bf16[512,768]{1,0:T(8,128)(2,1)}, bf16[512,768]{1,0:T(8,128)(2,1)}, u32[]{:S(2)}, u32[]{:S(2)}) collective-permute-start(bf16[512,768]{1,0:T(8,128)(2,1)} %shard_map.213.dep_ref), channel_id=1, source_target_pairs={{0,8},{24,16},{1,9},{25,17},{2,10},{26,18},{3,11},{27,19},{4,12},{... | collective-permute-start | bytes 2359304 | tf_op jit(solution)/shard_map/ppermute | solution.py:559
  185.7 43.5 %collective-permute-start.5 = (bf16[512,768]{1,0:T(8,128)(2,1)}, bf16[512,768]{1,0:T(8,128)(2,1)}, u32[]{:S(2)}, u32[]{:S(2)}) collective-permute-start(bf16[512,768]{1,0:T(8,128)(2,1)} %shard_map.214), channel_id=1, source_target_pairs={{0,8},{24,16},{1,9},{25,17},{2,10},{26,18},{3,11},{27,19},{4,12},{... | collective-permute-start | bytes 2359304 | tf_op jit(solution)/shard_map/ppermute | solution.py:559
  190.3 52.2 %all-to-all-start.4 = ((bf16[8,96,768]{2,1,0:T(8,128)(2,1)}), bf16[8,96,768]{2,1,0:T(8,128)(2,1)}, u32[]{:S(2)}, u32[]{:S(2)}) async-start(bf16[8,96,768]{2,1,0:T(8,128)(2,1)} %bitcast.9), calls=%async_computation.4 | async-start | bytes 2359296 | tf_op jit(solution)/shard_map/all_to_all | solution.py:516
  222.5 45.4 %collective-permute-start.6 = (bf16[512,768]{1,0:T(8,128)(2,1)}, bf16[512,768]{1,0:T(8,128)(2,1)}, u32[]{:S(2)}, u32[]{:S(2)}) collective-permute-start(bf16[512,768]{1,0:T(8,128)(2,1)} %add_convert_fusion.20), channel_id=1, source_target_pairs={{8,16},{16,8},{9,17},{17,9},{10,18},{18,10},{11,19},{19,11},{12,20... | collective-permute-start | bytes 2359304 | tf_op jit(solution)/shard_map/ppermute | solution.py:563
  224.1 112.0 %collective-permute-start.27 = (bf16[512,768]{1,0:T(8,128)(2,1)}, bf16[512,768]{1,0:T(8,128)(2,1)}, u32[]{:S(2)}, u32[]{:S(2)}) collective-permute-start(bf16[512,768]{1,0:T(8,128)(2,1)} %add_convert_fusion.21.rest_0_.a_ref), channel_id=1, source_target_pairs={{8,0},{16,24},{9,1},{17,25},{10,2},{18,26},{11,3},{19,27},{12,4},{... | collective-permute-start | bytes 2359304 | tf_op jit(solution)/shard_map/ppermute | solution.py:568
  227.9 142.9 %collective-permute-start.26 = (bf16[512,768]{1,0:T(8,128)(2,1)}, bf16[512,768]{1,0:T(8,128)(2,1)}, u32[]{:S(2)}, u32[]{:S(2)}) collective-permute-start(bf16[512,768]{1,0:T(8,128)(2,1)} %add_convert_fusion.19.a_ref), channel_id=1, source_target_pairs={{8,0},{16,24},{9,1},{17,25},{10,2},{18,26},{11,3},{19,27},{12,4},{... | collective-permute-start | bytes 2359304 | tf_op jit(solution)/shard_map/ppermute | solution.py:568
  231.6 68.9 %collective-permute-start.8 = (bf16[512,768]{1,0:T(8,128)(2,1)}, bf16[512,768]{1,0:T(8,128)(2,1)}, u32[]{:S(2)}, u32[]{:S(2)}) collective-permute-start(bf16[512,768]{1,0:T(8,128)(2,1)} %add_convert_fusion.18.rest_0_), channel_id=1, source_target_pairs={{8,16},{16,8},{9,17},{17,9},{10,18},{18,10},{11,19},{19,11},{12,20... | collective-permute-start | bytes 2359304 | tf_op jit(solution)/shard_map/ppermute | solution.py:563
  233.2 39.6 %collective-permute-start.7 = (bf16[512,768]{1,0:T(8,128)(2,1)}, bf16[512,768]{1,0:T(8,128)(2,1)}, u32[]{:S(2)}, u32[]{:S(2)}) collective-permute-start(bf16[512,768]{1,0:T(8,128)(2,1)} %shard_map.216), channel_id=1, source_target_pairs={{0,8},{24,16},{1,9},{25,17},{2,10},{26,18},{3,11},{27,19},{4,12},{... | collective-permute-start | bytes 2359304 | tf_op jit(solution)/shard_map/ppermute | solution.py:559
  267.9 36.5 %collective-permute-start.10 = (bf16[512,768]{1,0:T(8,128)(2,1)}, bf16[512,768]{1,0:T(8,128)(2,1)}, u32[]{:S(2)}, u32[]{:S(2)}) collective-permute-start(bf16[512,768]{1,0:T(8,128)(2,1)} %shard_map.217), channel_id=1, source_target_pairs={{0,8},{24,16},{1,9},{25,17},{2,10},{26,18},{3,11},{27,19},{4,12},{... | collective-permute-start | bytes 2359304 | tf_op jit(solution)/shard_map/ppermute | solution.py:559
  275.3 37.8 %collective-permute-start.11 = (bf16[512,768]{1,0:T(8,128)(2,1)}, bf16[512,768]{1,0:T(8,128)(2,1)}, u32[]{:S(2)}, u32[]{:S(2)}) collective-permute-start(bf16[512,768]{1,0:T(8,128)(2,1)} %add_convert_fusion.16.dep_ref), channel_id=1, source_target_pairs={{8,16},{16,8},{9,17},{17,9},{10,18},{18,10},{11,19},{19,11},{12,20... | collective-permute-start | bytes 2359304 | tf_op jit(solution)/shard_map/ppermute | solution.py:563
  300.5 110.9 %collective-permute-start.25 = (bf16[512,768]{1,0:T(8,128)(2,1)}, bf16[512,768]{1,0:T(8,128)(2,1)}, u32[]{:S(2)}, u32[]{:S(2)}) collective-permute-start(bf16[512,768]{1,0:T(8,128)(2,1)} %add_convert_fusion.17.a_ref), channel_id=1, source_target_pairs={{8,0},{16,24},{9,1},{17,25},{10,2},{18,26},{11,3},{19,27},{12,4},{... | collective-permute-start | bytes 2359304 | tf_op jit(solution)/shard_map/ppermute | solution.py:568
  313.2 29.3 %collective-permute-start.12 = (bf16[512,768]{1,0:T(8,128)(2,1)}, bf16[512,768]{1,0:T(8,128)(2,1)}, u32[]{:S(2)}, u32[]{:S(2)}) collective-permute-start(bf16[512,768]{1,0:T(8,128)(2,1)} %add_convert_fusion.13), channel_id=1, source_target_pairs={{8,16},{16,8},{9,17},{17,9},{10,18},{18,10},{11,19},{19,11},{12,20... | collective-permute-start | bytes 2359304 | tf_op jit(solution)/shard_map/ppermute | solution.py:563
  342.5 91.6 %collective-permute-start.24 = (bf16[512,768]{1,0:T(8,128)(2,1)}, bf16[512,768]{1,0:T(8,128)(2,1)}, u32[]{:S(2)}, u32[]{:S(2)}) collective-permute-start(bf16[512,768]{1,0:T(8,128)(2,1)} %add_convert_fusion.15.a_ref), channel_id=1, source_target_pairs={{8,0},{16,24},{9,1},{17,25},{10,2},{18,26},{11,3},{19,27},{12,4},{... | collective-permute-start | bytes 2359304 | tf_op jit(solution)/shard_map/ppermute | solution.py:568
  355.1 115.4 %collective-permute-start.23 = (bf16[512,768]{1,0:T(8,128)(2,1)}, bf16[512,768]{1,0:T(8,128)(2,1)}, u32[]{:S(2)}, u32[]{:S(2)}) collective-permute-start(bf16[512,768]{1,0:T(8,128)(2,1)} %add_convert_fusion.12.dep_ref.a_ref), channel_id=1, source_target_pairs={{8,0},{16,24},{9,1},{17,25},{10,2},{18,26},{11,3},{19,27},{12,4},{... | collective-permute-start | bytes 2359304 | tf_op jit(solution)/shard_map/ppermute | solution.py:568
  380.8 93.6 %collective-permute-start.22 = (bf16[512,768]{1,0:T(8,128)(2,1)}, bf16[512,768]{1,0:T(8,128)(2,1)}, u32[]{:S(2)}, u32[]{:S(2)}) collective-permute-start(bf16[512,768]{1,0:T(8,128)(2,1)} %add_convert_fusion.11.a_ref), channel_id=1, source_target_pairs={{8,0},{16,24},{9,1},{17,25},{10,2},{18,26},{11,3},{19,27},{12,4},{... | collective-permute-start | bytes 2359304 | tf_op jit(solution)/shard_map/ppermute | solution.py:568
  407.1 105.5 %all-to-all-start.6 = ((bf16[8,96,768]{2,1,0:T(8,128)(2,1)}), bf16[8,96,768]{2,1,0:T(8,128)(2,1)}, u32[]{:S(2)}, u32[]{:S(2)}) async-start(bf16[8,96,768]{2,1,0:T(8,128)(2,1)} %bitcast.14), calls=%async_computation.6 | async-start | bytes 2359296 | tf_op jit(solution)/shard_map/all_to_all | solution.py:516
  415.3 71.7 %collective-permute-start.21 = (bf16[512,768]{1,0:T(8,128)(2,1)}, bf16[512,768]{1,0:T(8,128)(2,1)}, u32[]{:S(2)}, u32[]{:S(2)}) collective-permute-start(bf16[512,768]{1,0:T(8,128)(2,1)} %add_convert_fusion.9.dep_ref.a_ref), channel_id=1, source_target_pairs={{8,0},{16,24},{9,1},{17,25},{10,2},{18,26},{11,3},{19,27},{12,4},{... | collective-permute-start | bytes 2359304 | tf_op jit(solution)/shard_map/ppermute | solution.py:568
  419.2 65.4 %collective-permute-start.28 = (bf16[512,768]{1,0:T(8,128)(2,1)}, bf16[512,768]{1,0:T(8,128)(2,1)}, u32[]{:S(2)}, u32[]{:S(2)}) collective-permute-start(bf16[512,768]{1,0:T(8,128)(2,1)} %add_convert_fusion.5), channel_id=1, source_target_pairs={{8,16},{16,8},{9,17},{17,9},{10,18},{18,10},{11,19},{19,11},{12,20... | collective-permute-start | bytes 2359304 | tf_op jit(solution)/shard_map/ppermute | solution.py:563
  434.1 32.4 %collective-permute-start.17 = (bf16[512,768]{1,0:T(8,128)(2,1)}, bf16[512,768]{1,0:T(8,128)(2,1)}, u32[]{:S(2)}, u32[]{:S(2)}) collective-permute-start(bf16[512,768]{1,0:T(8,128)(2,1)} %shard_map.224.rest_2_), channel_id=1, source_target_pairs={{0,8},{24,16},{1,9},{25,17},{2,10},{26,18},{3,11},{27,19},{4,12},{... | collective-permute-start | bytes 2359304 | tf_op jit(solution)/shard_map/ppermute | solution.py:559
  470.4 30.1 %collective-permute-start.30 = (bf16[512,768]{1,0:T(8,128)(2,1)}, bf16[512,768]{1,0:T(8,128)(2,1)}, u32[]{:S(2)}, u32[]{:S(2)}) collective-permute-start(bf16[512,768]{1,0:T(8,128)(2,1)} %add_convert_fusion.6.rest_2_), channel_id=1, source_target_pairs={{8,16},{16,8},{9,17},{17,9},{10,18},{18,10},{11,19},{19,11},{12,20... | collective-permute-start | bytes 2359304 | tf_op jit(solution)/shard_map/ppermute | solution.py:563
  516.2 61.6 %reduce-scatter.2.cloned.1.call-start = ((), (), s32[]{:S(2)}) async-start(), calls=%async_computation.8 | async-start | bytes 5529600 | tf_op jit(solution)/shard_map/reduce_scatter | solution.py:588
  517.0 105.5 %all-reduce.3.cloned.1.call-start = ((), (), s32[]{:S(2)}) async-start(), calls=%async_computation.9 | async-start | bytes 1228800 | tf_op jit(solution)/shard_map/psum | solution.py:590
  517.0 44.4 %collective-permute-start.34 = (bf16[512,768]{1,0:T(8,128)(2,1)}, bf16[512,768]{1,0:T(8,128)(2,1)}, u32[]{:S(2)}, u32[]{:S(2)}) collective-permute-start(bf16[512,768]{1,0:T(8,128)(2,1)} %add_convert_fusion.3.rest_2_.a_ref), channel_id=1, source_target_pairs={{8,0},{16,24},{9,1},{17,25},{10,2},{18,26},{11,3},{19,27},{12,4},{... | collective-permute-start | bytes 2359304 | tf_op jit(solution)/shard_map/ppermute | solution.py:568
  518.5 39.3 %collective-permute-start.35 = (bf16[512,768]{1,0:T(8,128)(2,1)}, bf16[512,768]{1,0:T(8,128)(2,1)}, u32[]{:S(2)}, u32[]{:S(2)}) collective-permute-start(bf16[512,768]{1,0:T(8,128)(2,1)} %add_convert_fusion.4.dep_ref.a_ref), channel_id=1, source_target_pairs={{8,0},{16,24},{9,1},{17,25},{10,2},{18,26},{11,3},{19,27},{12,4},{... | collective-permute-start | bytes 2359304 | tf_op jit(solution)/shard_map/ppermute | solution.py:568
  519.8 58.1 %collective-permute-start.33 = (bf16[512,768]{1,0:T(8,128)(2,1)}, bf16[512,768]{1,0:T(8,128)(2,1)}, u32[]{:S(2)}, u32[]{:S(2)}) collective-permute-start(bf16[512,768]{1,0:T(8,128)(2,1)} %add_convert_fusion.1.refs_2_.a_ref), channel_id=1, source_target_pairs={{8,0},{16,24},{9,1},{17,25},{10,2},{18,26},{11,3},{19,27},{12,4},{... | collective-permute-start | bytes 2359304 | tf_op jit(solution)/shard_map/ppermute | solution.py:568
  523.5 99.0 %collective-permute-start.32 = (bf16[512,768]{1,0:T(8,128)(2,1)}, bf16[512,768]{1,0:T(8,128)(2,1)}, u32[]{:S(2)}, u32[]{:S(2)}) collective-permute-start(bf16[512,768]{1,0:T(8,128)(2,1)} %add_convert_fusion.dep_ref.a_ref), channel_id=1, source_target_pairs={{8,0},{16,24},{9,1},{17,25},{10,2},{18,26},{11,3},{19,27},{12,4},{... | collective-permute-start | bytes 2359304 | tf_op jit(solution)/shard_map/ppermute | solution.py:568
  577.8 86.2 %all-gather.2.cloned.1.call-start = ((), (), s32[]{:S(2)}) async-start(), calls=%async_computation.10 | async-start | bytes 5529600 | tf_op jit(solution)/shard_map/all_gather | solution.py:592
  (128 other events, 843.5 us)
Sparse Core Ops, SparseCore 0:
  520.5 57.1 reduce-scatter.1
  580.2 42.1 all-reduce.2
  624.5 39.4 all-gather.1
